TPU v7x, 32 devices: a whole 2x2x4 slice. The times are simulated.
32 devices in a mesh: dp: 4 (over z), stage: 2 (over y), tp: 4 (over x, core).
Axes of the slice: x: 2, y: 2, z: 4, core: 2. Of those that a mesh axis runs over, the one named last changes fastest.
Arguments:
- act_in: bfloat16 [2, 16, 28, 28, 512], P('stage', ('dp', 'tp'))
- w_conv: bfloat16 [2, 3, 3, 512, 512], P('stage', None, None, 'tp')
- w_short: bfloat16 [2, 512, 512], P('stage', 'tp')
- gamma: float32 [2, 512], P('stage', 'tp')
- beta: float32 [2, 512], P('stage', 'tp')
- gamma_s: float32 [2, 512], P('stage', 'tp')
- grad_z: bfloat16 [2, 16, 28, 28, 512], P('stage', 'dp', None, None, 'tp')
Outputs:
- output 1: bfloat16 [2, 16, 28, 28, 512], P('stage', 'dp', None, None, 'tp')
- output 2: bfloat16 [2, 16, 28, 28, 512], P('stage', ('dp', 'tp'))
- output 3: float32 [2, 3, 3, 512, 512], P('stage', None, None, 'tp')
- output 4: float32 [2, 512, 512], P('stage', 'tp')
All inputs are finite; a program needn't handle non-finite values.
Results may differ from a plain program's by a relative error of at most 0.00599.
Values are sent between devices in bfloat16 or wider.
A program may use at most 1 GiB of HBM per device.

v0:
```python
import jax
import jax.numpy as jnp
from jax import lax
from jax.sharding import PartitionSpec as P


def conv_same(left_op, right_op, right_spec):
    return lax.conv_general_dilated(left_op, right_op, (1, 1), "SAME", dimension_numbers=("NHWC", right_spec, "NHWC"), preferred_element_type=jnp.float32)


def weight_grad(images_in, grads_out):
    return lax.conv_general_dilated(images_in, grads_out, (1, 1), ((1, 1), (1, 1)), dimension_numbers=("CHWN", "IHWO", "HWNC"), preferred_element_type=jnp.float32)


def solution(mesh):
    act_spec = P("stage", ("dp", "tp"), None, None, None)
    kernel_spec = P("stage", None, None, "tp", None)
    short_spec = P("stage", "tp", None)
    vec_spec = P("stage", "tp")
    grad_spec = P("stage", "dp", None, None, "tp")

    def device_step(act_in, w_conv, w_short, gamma, beta, gamma_s, grad_z):
        by_channel = lax.all_to_all(act_in[0], "tp", 3, 0, tiled=True)
        act_local = lax.ppermute(by_channel, "stage", perm=[(0, 1)])
        kernel = w_conv[0]
        short_w = w_short[0]
        scale_main = gamma[0]
        shift_main = beta[0]
        scale_short = gamma_s[0]
        pre_part = conv_same(act_local, kernel, "HWIO")
        short_part = jnp.einsum("nhwc,co->nhwo", act_local, short_w, preferred_element_type=jnp.float32)
        pre_sum, short_sum = lax.psum_scatter((pre_part, short_part), "tp", scatter_dimension=3, tiled=True)
        mixed_sum = pre_sum * scale_main + shift_main + short_sum * scale_short
        z_val = jnp.maximum(mixed_sum, 0.0).astype(jnp.bfloat16)
        mask_pos = mixed_sum > 0.0
        grad_here = grad_z[0]
        g_main = jnp.where(mask_pos, grad_here * scale_main, 0.0).astype(jnp.bfloat16)
        g_short = jnp.where(mask_pos, grad_here * scale_short, 0.0).astype(jnp.bfloat16)
        g_main_all, g_short_all = lax.all_gather((g_main, g_short), "tp", axis=3, tiled=True)
        grad_wide = conv_same(g_main_all, kernel[::-1, ::-1], "HWOI") + jnp.einsum("nhwo,co->nhwc", g_short_all, short_w, preferred_element_type=jnp.float32)
        grad_local = grad_wide.astype(jnp.bfloat16)
        dw_part = weight_grad(act_local, g_main_all)
        dws_part = jnp.einsum("nhwc,nhwo->co", act_local, g_short_all, preferred_element_type=jnp.float32)
        dw_sum, dws_sum = lax.psum((dw_part, dws_part), "dp")
        returned = lax.ppermute(grad_local, "stage", perm=[(1, 0)])
        grad_act = lax.all_to_all(returned, "tp", 0, 3, tiled=True)
        return z_val[None], grad_act[None], dw_sum[None], dws_sum[None]

    return jax.shard_map(device_step, mesh=mesh, in_specs=(act_spec, kernel_spec, short_spec, vec_spec, vec_spec, vec_spec, grad_spec), out_specs=(grad_spec, act_spec, kernel_spec, short_spec), check_vma=False)
```

profile of v0, /device:TPU:0, one launch (start us, length us, event | category | flops | bytes accessed | tf_op | source)
XLA Modules:
  0.0 426.6 jit_solution(12278056099545943415)
XLA Ops:
  7.2 0.0 copy-start
  7.2 0.0 reduce-scatter.3.cloned.1.call-start
  7.2 8.3 %copy.54 = bf16[1,1,28,28,512]{3,2,4,1,0:T(8,128)(2,1)} copy(bf16[1,1,28,28,512]{4,3,2,1,0:T(8,128)(2,1)} %param.7) | data formatting | bytes 1605632 | tf_op args[0]
  15.5 4.8 %bitcast_bitcast_fusion = bf16[512,1,28,28]{3,2,1,0:T(8,128)(2,1)} fusion(bf16[1,1,28,28,512]{3,2,4,1,0:T(8,128)(2,1)} %copy.54), kind=kLoop, calls=%fused_computation.46 | loop fusion | bytes 1605632
  20.4 6.1 %reshape.37 = bf16[4,2,50176]{2,1,0:T(2,128)(2,1)S(1)} reshape(bf16[512,1,28,28]{3,2,1,0:T(8,128)(2,1)} %bitcast_bitcast_fusion) | data formatting | bytes 1605632
  26.4 15.9 %all_to_all.33 = bf16[4,2,50176]{2,1,0:T(2,128)(2,1)S(1)} all-to-all(bf16[4,2,50176]{2,1,0:T(2,128)(2,1)S(1)} %reshape.37), channel_id=1, replica_groups=mesh['dp'=4,'stage'=2,'tp'=4] {'tp'}, dimensions={0} | all-to-all | bytes 1605632 | tf_op jit(solution)/shard_map/all_to_all | solution.py:23
  42.3 5.0 %reshape.38 = bf16[512,1,28,28]{3,2,1,0:T(8,128)(2,1)} reshape(bf16[4,2,50176]{2,1,0:T(2,128)(2,1)S(1)} %all_to_all.33) | data formatting | bytes 1605632
  47.3 5.6 %copy.75 = bf16[1,28,28,4,128]{4,3,2,1,0:T(4,128)(2,1)S(1)} copy(bf16[1,28,28,4,128]{2,1,4,3,0:T(8,128)(2,1)} %bitcast.71) | data formatting | bytes 1605632 | tf_op jit(solution)/shard_map/all_to_all | solution.py:23
  52.9 0.0 copy-start.10
  52.9 3.6 collective-permute-start
  56.6 17.1 %collective-permute-done = bf16[4,28,28,128]{3,0,2,1:T(4,128)(2,1)S(1)} collective-permute-done((bf16[4,28,28,128]{3,0,2,1:T(4,128)(2,1)S(1)}, bf16[4,28,28,128]{3,0,2,1:T(4,128)(2,1)S(1)}, u32[]{:S(2)}, u32[]{:S(2)}) %collective-permute-start) | collective-permute-done | bytes 802848 | tf_op jit(solution)/shard_map/ppermute | solution.py:24
  73.6 0.5 pad
  74.1 0.4 copy.57
  74.5 0.1 slice.4
  74.6 0.0 copy-done
  74.7 0.0 copy-done.10
  74.7 4.9 %broadcast_select_fusion = f32[28,32,4,512]{3,1,2,0:T(8,128)S(1)} fusion(pred[32,4]{0,1:T(4,128)(4,1)S(1)} %copy-done.10, bf16[28,4,7,2,128]{4,2,1,3,0:T(8,128)(2,1)S(1)} %slice.4, bf16[28,4,8,4,128]{4,2,1,3,0:T(8,128)(2,1)S(1)} %copy.57, bf16[1,3,3,128,512]{4,3,2,1,0:T(8,128)(2,1)S(1)} %copy-done), kind=kOutput, calls=%fused_computation.9 | convolution fusion | flops 4133158912 | bytes 9838720 | tf_op jit(solution)/shard_map/conv_general_dilated | solution.py:8
  79.6 9.0 %copy.58 = f32[28,32,4,512]{3,2,1,0:T(4,128)} copy(f32[28,32,4,512]{3,1,2,0:T(8,128)S(1)} %broadcast_select_fusion) | data formatting | bytes 14680064 | tf_op jit(solution)/shard_map/conv_general_dilated | solution.py:8
  88.6 9.8 %reshape.20 = f32[28,4,32,512]{3,2,1,0:T(8,128)} reshape(f32[28,32,4,512]{3,2,1,0:T(4,128)} %copy.58) | data formatting | bytes 14680064 | tf_op jit(solution)/shard_map/conv_general_dilated | solution.py:8
  98.4 7.6 %copy_bitcast_fusion = f32[4,28,28,512]{3,2,1,0:T(8,128)} fusion(f32[28,4,32,512]{3,2,1,0:T(8,128)} %reshape.20), kind=kLoop, calls=%fused_computation.3 | loop fusion | bytes 13762560 | tf_op jit(solution)/shard_map/conv_general_dilated | solution.py:8
  106.1 0.0 reduce-scatter.3.cloned.1.call-update
  106.1 0.0 reduce-scatter.5.cloned.1.call-start
  106.1 0.8 copy-done.5
  107.0 4.1 fusion.35
  111.1 0.0 reduce-scatter.5.cloned.1.call-update
  111.1 0.0 all-gather.3.cloned.1.call-start
  111.2 59.7 %reduce-scatter.3.cloned.1.call-done = f32[4,28,28,128]{3,2,1,0:T(8,128)} async-done(((f32[4,28,28,512]{3,2,1,0:T(8,128)}), f32[4,28,28,128]{3,2,1,0:T(8,128)}) %reduce-scatter.3.cloned.1.call-update) | async-done | bytes 1605648 | tf_op jit(solution)/shard_map/reduce_scatter | solution.py:32
  170.9 65.9 %reduce-scatter.5.cloned.1.call-done = f32[4,28,28,128]{3,2,1,0:T(8,128)} async-done(((f32[4,28,28,512]{3,2,1,0:T(8,128)}), f32[4,28,28,128]{3,2,1,0:T(8,128)}) %reduce-scatter.5.cloned.1.call-update) | async-done | bytes 1605648 | tf_op jit(solution)/shard_map/reduce_scatter | solution.py:32
  236.8 0.0 copy-done.4
  236.8 0.0 copy-done.8
  236.8 4.2 fusion.13
  241.0 1.3 fusion.11
  242.2 0.0 all-gather.3.cloned.1.call-update
  242.3 0.0 all-gather.5.cloned.1.call-start
  242.3 0.5 all-gather.5.cloned.1.call-update
  242.9 0.0 all-reduce.3.cloned.1.call-start
  242.9 31.3 %all-gather.3.cloned.1.call-done = bf16[4,28,28,512]{3,2,1,0:T(8,128)(2,1)} async-done(((bf16[4,28,28,128]{3,2,1,0:T(8,128)(2,1)}), bf16[4,28,28,512]{3,2,1,0:T(8,128)(2,1)}) %all-gather.3.cloned.1.call-update) | async-done | bytes 3211280 | tf_op jit(solution)/shard_map/all_gather | solution.py:39
  274.2 11.8 %fusion.16 = f32[1,3,3,128,512]{4,3,2,1,0:T(8,128)} fusion(bf16[4,28,28,128]{3,0,2,1:T(4,128)(2,1)S(1)} %collective-permute-done, bf16[4,28,28,512]{3,2,1,0:T(8,128)(2,1)} %all-gather.3.cloned.1.call-done), kind=kOutput, calls=%fused_computation.25 | convolution fusion | flops 3525312512 | bytes 6373376 | tf_op jit(solution)/shard_map/conv_general_dilated | solution.py:12
  285.9 4.0 pad.2
  290.0 6.7 %reshape.23 = bf16[28,4,8,4,512]{4,3,2,0,1:T(4,128)(2,1)} reshape(bf16[28,4,32,512]{3,2,0,1:T(8,128)(2,1)} %pad.2) | data formatting | bytes 7340032 | tf_op jit(solution)/shard_map/conv_general_dilated | solution.py:8
  296.7 3.0 slice.6
  299.7 7.3 %fusion.1 = bf16[28,4,8,6,512]{4,3,2,0,1:T(8,128)(2,1)} fusion(bf16[28,4,7,2,512]{4,3,2,0,1:T(2,128)(2,1)S(1)} %slice.6, bf16[28,4,8,4,512]{4,3,2,0,1:T(4,128)(2,1)} %reshape.23), kind=kLoop, calls=%fused_computation.2 | loop fusion | flops 16515072 | bytes 10780672 | tf_op jit(solution)/shard_map/conv_general_dilated | solution.py:8
  307.0 0.9 all-gather.5.cloned.1.call-done
  307.9 3.9 fusion.30
  311.8 0.0 all-reduce.3.cloned.1.call-update
  311.8 0.0 copy-done.11
  311.8 0.0 copy-start.6
  311.8 14.0 %fusion.19 = f32[28,32,4,128]{3,1,2,0:T(8,128)S(1)} fusion(bf16[28,4,8,6,512]{4,3,2,0,1:T(8,128)(2,1)} %fusion.1, bf16[1,3,3,128,512]{4,3,2,1,0:T(8,128)(2,1)S(1)} %copy-done, pred[32,4]{0,1:T(4,128)(4,1)S(1)} %copy-done.11), kind=kOutput, calls=%fused_computation.26 | convolution fusion | flops 4127653888 | bytes 8519808 | tf_op jit(solution)/shard_map/conv_general_dilated | solution.py:8
  325.9 0.0 copy-start.1
  325.9 1.6 copy.63
  327.4 0.5 copy-done.1
  327.9 1.1 fusion.15
  329.0 0.6 copy.65
  329.6 1.3 collective-permute-start.1
  330.9 20.6 %collective-permute-done.1 = bf16[4,28,28,128]{3,0,2,1:T(4,128)(2,1)S(1)} collective-permute-done((bf16[4,28,28,128]{3,0,2,1:T(4,128)(2,1)S(1)}, bf16[4,28,28,128]{3,0,2,1:T(4,128)(2,1)S(1)}, u32[]{:S(2)}, u32[]{:S(2)}) %collective-permute-start.1) | collective-permute-done | bytes 802848 | tf_op jit(solution)/shard_map/ppermute | solution.py:45
  351.6 1.1 copy.66
  352.6 3.5 all-to-all-start.1
  356.2 1.5 copy.71
  357.7 11.3 %all-to-all-done.1 = bf16[4,28,28,128]{3,2,1,0:T(8,128)(2,1)S(1)} async-done(((bf16[4,28,28,128]{3,2,1,0:T(8,128)(2,1)}), bf16[4,28,28,128]{3,2,1,0:T(8,128)(2,1)S(1)}, u32[]{:S(2)}, u32[]{:S(2)}) %all-to-all-start.1) | async-done | bytes 802848 | tf_op jit(solution)/shard_map/all_to_all | solution.py:46
  368.9 0.6 copy.67
  369.6 1.2 broadcast_in_dim.16
  370.8 44.0 %all-reduce.3.cloned.1.call-done = (f32[1,3,3,128,512]{4,3,2,1,0:T(8,128)}, f32[1,128,512]{1,2,0:T(8,128)}) async-done(((f32[1,3,3,128,512]{4,3,2,1,0:T(8,128)}, f32[1,128,512]{1,2,0:T(8,128)}), (f32[1,3,3,128,512]{4,3,2,1,0:T(8,128)}, f32[1,128,512]{1,2,0:T(8,128)})) %all-reduce.3.cloned.1.call-update) | async-done | bytes 2621456 | tf_op jit(solution)/shard_map/psum | solution.py:44
  414.8 1.8 copy.72
  416.6 3.3 copy.106
  (13 shorter events, 0.0 us)
Async XLA Ops:
  7.2 67.5 %copy-start = (bf16[1,3,3,128,512]{4,3,2,1,0:T(8,128)(2,1)S(1)}, bf16[1,3,3,128,512]{4,3,2,1,0:T(8,128)(2,1)}, u32[]{:S(2)}) copy-start(bf16[1,3,3,128,512]{4,3,2,1,0:T(8,128)(2,1)} %param.8) | copy-start | bytes 3538948
  7.2 163.7 %reduce-scatter.3.cloned.1.call-start = ((), (), s32[]{:S(2)}) async-start(), calls=%async_computation.4 | async-start | bytes 9175040 | tf_op jit(solution)/shard_map/reduce_scatter | solution.py:32
  52.9 21.8 %copy-start.10 = (pred[32,4]{0,1:T(4,128)(4,1)S(1)}, pred[32,4]{0,1:T(4,128)(4,1)}, u32[]{:S(2)}) copy-start(pred[32,4]{0,1:T(4,128)(4,1)} %constant.18) | copy-start | bytes 388
  52.9 20.7 %collective-permute-start = (bf16[4,28,28,128]{3,0,2,1:T(4,128)(2,1)S(1)}, bf16[4,28,28,128]{3,0,2,1:T(4,128)(2,1)S(1)}, u32[]{:S(2)}, u32[]{:S(2)}) collective-permute-start(bf16[4,28,28,128]{3,0,2,1:T(4,128)(2,1)S(1)} %bitcast.77), channel_id=1, source_target_pairs={{0,4},{1,5},{2,6},{3,7},{8,12},{9,13},{10,14},{11,15},{16,20},{17,... | collective-permute-start | bytes 2408456 | tf_op jit(solution)/shard_map/ppermute | solution.py:24
  106.1 0.9 copy-start.5
  106.1 130.7 %reduce-scatter.5.cloned.1.call-start = ((), (), s32[]{:S(2)}) async-start(), calls=%async_computation.5 | async-start | bytes 9175040 | tf_op jit(solution)/shard_map/reduce_scatter | solution.py:32
  111.1 125.7 %copy-start.4 = (bf16[1,4,28,28,128]{4,1,3,2,0:T(4,128)(2,1)S(1)}, bf16[1,4,28,28,128]{4,1,3,2,0:T(4,128)(2,1)}, u32[]{:S(2)}) copy-start(bf16[1,4,28,28,128]{4,1,3,2,0:T(4,128)(2,1)} %param.13) | copy-start | bytes 2408452
  111.1 125.7 %copy-start.7 = (f32[1,128]{1,0:T(1,128)S(1)}, f32[1,128]{1,0:T(1,128)}, u32[]{:S(2)}) copy-start(f32[1,128]{1,0:T(1,128)} %param.10) | copy-start | bytes 1540
  111.1 125.7 %copy-start.8 = (f32[1,128]{1,0:T(1,128)S(1)}, f32[1,128]{1,0:T(1,128)}, u32[]{:S(2)}) copy-start(f32[1,128]{1,0:T(1,128)} %param.12) | copy-start | bytes 1540
  111.1 125.7 %copy-start.9 = (f32[1,128]{1,0:T(1,128)S(1)}, f32[1,128]{1,0:T(1,128)}, u32[]{:S(2)}) copy-start(f32[1,128]{1,0:T(1,128)} %param.11) | copy-start | bytes 1540
  111.1 163.0 %all-gather.3.cloned.1.call-start = ((), (), s32[]{:S(2)}) async-start(), calls=%async_computation.6 | async-start | bytes 4587520 | tf_op jit(solution)/shard_map/all_gather | solution.py:39
  242.3 65.6 %all-gather.5.cloned.1.call-start = ((), (), s32[]{:S(2)}) async-start(), calls=%async_computation.7 | async-start | bytes 4587520 | tf_op jit(solution)/shard_map/all_gather | solution.py:39
  242.9 172.0 %all-reduce.3.cloned.1.call-start = ((), (), s32[]{:S(2)}) async-start(), calls=%async_computation.8 | async-start | bytes 5242880 | tf_op jit(solution)/shard_map/psum | solution.py:44
  274.2 11.8 %copy-start.2 = (bf16[4,28,28,512]{3,2,1,0:T(8,128)(2,1)S(1)}, bf16[4,28,28,512]{3,2,1,0:T(8,128)(2,1)}, u32[]{:S(2)}) copy-start(bf16[4,28,28,512]{3,2,1,0:T(8,128)(2,1)} %all-gather.3.cloned.1.call-done) | copy-start | bytes 9633796
  307.0 4.9 %copy-start.11 = (pred[32,4]{0,1:T(4,128)(4,1)S(1)}, pred[32,4]{0,1:T(4,128)(4,1)}, u32[]{:S(2)}) copy-start(pred[32,4]{0,1:T(4,128)(4,1)} %constant.18) | copy-start | bytes 388
  311.8 15.6 %copy-start.6 = (bf16[1,128,512]{2,1,0:T(8,128)(2,1)S(1)}, bf16[1,128,512]{2,1,0:T(8,128)(2,1)}, u32[]{:S(2)}) copy-start(bf16[1,128,512]{2,1,0:T(8,128)(2,1)} %param.9) | copy-start | bytes 393220
  325.9 2.0 copy-start.1
  329.0 27.2 %copy-start.3 = (bf16[1,4,28,28,128]{4,3,2,1,0:T(8,128)(2,1)S(1)}, bf16[1,4,28,28,128]{4,3,2,1,0:T(8,128)(2,1)}, u32[]{:S(2)}) copy-start(bf16[1,4,28,28,128]{4,3,2,1,0:T(8,128)(2,1)} %get-tuple-element.24) | copy-start | bytes 2408452
  329.6 21.9 %collective-permute-start.1 = (bf16[4,28,28,128]{3,0,2,1:T(4,128)(2,1)S(1)}, bf16[4,28,28,128]{3,0,2,1:T(4,128)(2,1)S(1)}, u32[]{:S(2)}, u32[]{:S(2)}) collective-permute-start(bf16[4,28,28,128]{3,0,2,1:T(4,128)(2,1)S(1)} %copy.65), channel_id=1, source_target_pairs={{4,0},{5,1},{6,2},{7,3},{12,8},{13,9},{14,10},{15,11},{20,16},{21,... | collective-permute-start | bytes 2408456 | tf_op jit(solution)/shard_map/ppermute | solution.py:45
  352.6 16.3 %all-to-all-start.1 = ((bf16[4,28,28,128]{3,2,1,0:T(8,128)(2,1)}), bf16[4,28,28,128]{3,2,1,0:T(8,128)(2,1)S(1)}, u32[]{:S(2)}, u32[]{:S(2)}) async-start(bf16[4,28,28,128]{3,2,1,0:T(8,128)(2,1)} %copy.66), calls=%async_computation.3 | async-start | bytes 1835008 | tf_op jit(solution)/shard_map/all_to_all | solution.py:46
Sparse Core Ops, SparseCore 0:
  106.2 64.6 reduce-scatter.2
  173.4 63.3 reduce-scatter.4
  242.4 31.7 all-gather.2
  276.1 31.7 all-gather.4
  311.9 102.8 all-reduce.2
where the time goes:
time: 432 us; the launch traced here: 427 us
  waiting for transfers between devices  251 us (58%)
  local copies, waits for them, and re-layouts  84 us (19%)
  matrix products  39.8 us (9%)
  blocking collectives  15.9 us (4%)
  between operations  14.2 us (3%)
  other arithmetic  12.7 us (3%)
  starting transfers between devices  8.65 us (2%)
    reduce_scatter x2, waiting for transfers between devices, device_step(): lax.psum_scatter((pre_part, short_part), 'tp', scatter_dimension=3, tiled...  126 us
    psum x1, waiting for transfers between devices, device_step(): dw_sum, dws_sum = lax.psum((dw_part, dws_part), 'dp')  44 us
    conv_general_dilated x8, local copies, waits for them, and re-layouts, conv_same(): lax.conv_general_dilated(left_op, right_op, (1, 1), 'SAME', dimension_num...  38.2 us
    all_gather x2, waiting for transfers between devices, device_step(): lax.all_gather((g_main, g_short), 'tp', axis=3, tiled=True)  32.2 us
    unnamed x31, local copies, waits for them, and re-layouts  32.1 us
    ppermute x1, waiting for transfers between devices, device_step(): returned = lax.ppermute(grad_local, 'stage', perm=[(1, 0)])  20.6 us
    conv_general_dilated x2, matrix products, conv_same(): lax.conv_general_dilated(left_op, right_op, (1, 1), 'SAME', dimension_num...  18.9 us
    ppermute x1, waiting for transfers between devices, device_step(): act_local = lax.ppermute(by_channel, 'stage', perm=[(0, 1)])  17.1 us
  transfers between devices with their start and end apart: 8, of which 8 were waited for; matrix products, arithmetic and copies ran while one was open for 14% of the time, Pallas kernels for 0%

commit v1 on v0

v1 whole, which is shorter than its diff:
```python
import jax
import jax.numpy as jnp
from jax import lax
from jax.experimental import pallas as pl
from jax.experimental.pallas import tpu as pltpu
from jax.sharding import PartitionSpec as P

BF = jnp.bfloat16
F32 = jnp.float32
MESH = pl.DeviceIdType.MESH
B = 128
C = 4 * B
W3 = 3 * B
IMGS = 4
HW = 28
WP = 32
HT = 7
NT = 4
M = HT * WP
NCROSS = 1
R = B // 2
NEAR = (0, 2)
MAIN = 1


def lanes(k):
    return pl.ds(pl.multiple_of(k * B, B), B)


def block_kernel(act, wc, ws, gam, bet, gams, gz, z_out, dx_out, dw_out, ds_out,
                 xl, x4, xt, w4, s4, wf, dzl, wide, d4, dzm, zf, zb, g4, part, pa, re, rm, tt, ff, fo, ob, obs,
                 w0, s0, ga, gsa, g0, gp, gsp, dxb, sem):
    dp = lax.axis_index("dp")
    st = lax.axis_index("stage")
    tp = lax.axis_index("tp")
    par = lax.rem(tp, 2)
    half = tp // 2
    sib = tp + 1 - 2 * par
    nbx = lax.rem(tp + 2, IMGS)
    dia = lax.rem(sib + 2, IMGS)

    def rc(src, dst, name, *k, land=None, **dev):
        ssem, rsem = sem["s" + name], sem["r" + name]
        return pltpu.make_async_remote_copy(src_ref=src, dst_ref=dst, send_sem=ssem.at[k], recv_sem=rsem.at[land or k], device_id=dev, device_id_type=MESH)

    def local(src, dst, k):
        return pltpu.make_async_copy(src, dst, sem["l"].at[k])

    def owner(o):
        return jnp.where(o == 0, tp, jnp.where(o == 1, sib, jnp.where(o == 2, nbx, dia)))

    is_end = jnp.logical_or(dp == 0, dp == 3)
    inner = jnp.where(dp == 0, 1, 2)

    def up(k, n):
        return rc(pa.at[k, :, pl.ds(0, n)], re.at[k, :, pl.ds(0, n)], "e", k, dp=inner)

    def send_up(ks, n, p_wait):
        @pl.when(is_end)
        def _():
            for k in ks:
                p_wait(k)
                up(k, n).start()

    def all_reduce(pairs, n, p_wait, emit):
        def cols(ref, k):
            return ref.at[k, :, pl.ds(0, n)]

        @pl.when(is_end)
        def _():
            for k in range(2 * pairs):
                rc(cols(ff, k), cols(ff, k), "h", k, dp=inner).wait_recv()
                emit(k)
            for k in range(2 * pairs):
                up(k, n).wait_send()

        @pl.when(jnp.logical_not(is_end))
        def _():
            endn = jnp.where(dp == 1, 0, 3)
            midn = 3 - dp

            def mine(m):
                return 2 * m + dp - 1

            def other(m):
                return 2 * m + 2 - dp

            def e_wait(k):
                rc(cols(pa, k), cols(re, k), "e", k, dp=endn).wait_recv()

            def to_root(m):
                return rc(cols(tt, m), cols(rm, m), "m", m, dp=midn)

            def to_mid(k):
                return rc(cols(ff, k), cols(ff, k), "f", k, dp=midn)

            def to_end(k):
                return rc(cols(ff, k), cols(ff, k), "h", k, dp=endn)

            def forward_result(m):
                k = other(m)
                rc(cols(ff, k), cols(ff, k), "f", k, dp=midn).wait_recv()
                to_end(k).start()
                emit(k)

            for m in range(pairs):
                k = other(m)
                p_wait(k)
                e_wait(k)
                tt[m, :, :n] = pa[k, :, :n] + re[k, :, :n]
                to_root(m).start()
                k = mine(m)
                p_wait(k)
                e_wait(k)
                to_root(m).wait_recv()
                ff[k, :, :n] = pa[k, :, :n] + re[k, :, :n] + rm[m, :, :n]
                to_end(k).start()
                to_mid(k).start()
                emit(k)
                if m > 0:
                    forward_result(m - 1)
            forward_result(pairs - 1)
            for m in range(pairs):
                to_root(m).wait_send()
                to_mid(mine(m)).wait_send()
                to_end(mine(m)).wait_send()
                to_end(other(m)).wait_send()

    @pl.when(st == 1)
    def _():
        def own_w(k, dst_k):
            return wc.at[:, :, :, lanes(k)], w4.at[:, :, lanes(dst_k)]

        def own_s(k, dst_k):
            return ws.at[:, lanes(k)], s4.at[lanes(dst_k)]

        loads = [local(gz, dzl, 0), local(*own_w(tp, tp), 1), local(*own_s(tp, tp), 2)]
        for c in loads:
            c.start()

        def w_copy(o):
            return rc(*own_w(owner(o), tp), "w", o, tp=owner(o))

        def s_copy(o):
            return rc(*own_s(owner(o), tp), "v", o, tp=owner(o))

        odd = lax.rem(dp, 2)
        peer = dp + 1 - 2 * odd

        def w_half(o, k, h):
            rows = pl.ds(k * B + h * R, R)
            return w4.at[:, :, rows], s4.at[rows]

        def far_copies(o):
            k = owner(o)
            mine = pl.ds(odd * R, R)
            dst_w, dst_s = w_half(o, tp, odd)
            return rc(wc.at[:, :, mine, lanes(k)], dst_w, "w", o, tp=k), rc(ws.at[mine, lanes(k)], dst_s, "v", o, tp=k)

        def far_recv(o):
            dst_w, dst_s = w_half(o, owner(o), odd)
            return rc(dst_w, dst_w, "w", o, tp=owner(o)), rc(dst_s, dst_s, "v", o, tp=owner(o))

        def peer_copies(o, h):
            dst_w, dst_s = w_half(o, owner(o), h)
            return rc(dst_w, dst_w, "i", o, dp=peer), rc(dst_s, dst_s, "j", o, dp=peer)

        far = (2, 3)
        w_sends = [*far_copies(2), *far_copies(3), w_copy(1), s_copy(1)]
        for c in w_sends:
            c.start()

        quarters = [rc(wc.at[i], w0.at[i, :, tp], "a", i, stage=0) for i in range(3)]
        quarters.append(rc(ws, s0.at[tp], "a", 3, stage=0))
        for o in range(IMGS):
            quarters.append(rc(gam, ga.at[tp], "y", o, stage=0, tp=owner(o)))
            quarters.append(rc(gams, gsa.at[tp], "u", o, stage=0, tp=owner(o)))
        for c in quarters:
            c.start()

        edge = jnp.zeros((WP, C), BF)
        for o in range(IMGS):
            for r in (0, HW + 1):
                x4[o, r] = edge
                g4[o, r] = edge
        x4[:, :, 24:, :] = jnp.zeros((IMGS, HW + 2, 8, C), BF)
        d4[:, :, 24:, :] = jnp.zeros((IMGS, HW, 8, B), BF)
        for i in NEAR:
            wf[i, :, W3:] = jnp.zeros((C, B), BF)

        loads[0].wait()
        wide[...] = dzl[...].astype(F32)

        def split_rows(h, c):
            for o in range(IMGS):
                d4[o, h, :HW, :] = wide[pl.ds(h * HW * IMGS + o, HW, stride=IMGS), :].astype(BF)
            return c

        lax.fori_loop(0, HW, split_rows, 0)

        scale_main = gam[...]
        shift_main = bet[...]
        scale_short = gams[...]

        def rows(img, k):
            return xl.at[img, pl.ds(k * HT, HT)]

        def land(o, k):
            img = owner(o)
            ref = rows(img, k)
            if o == 0:
                rc(ref, ref, "a", k, stage=0).wait_recv()
                rc(ref, ref, "b", k, tp=sib).start()

                @pl.when(k >= NCROSS)
                def _():
                    rc(ref, ref, "c", k, tp=nbx).start()
            elif o == 1:
                rc(ref, ref, "b", k, tp=sib).wait_recv()
            elif o == 2:
                rc(ref, ref, "c", k, tp=nbx).wait_recv()
                rc(ref, ref, "d", k, tp=sib).start()
            else:
                rc(ref, ref, "d", k, tp=sib).wait_recv()
            for r in range(HT):
                h = k * HT + r
                x4[img, 1 + h, :HW, :] = xl[img, h]

        def weights():
            for c in loads[1:]:
                c.wait()
            rc(*own_w(sib, sib), "w", 1, tp=sib).wait_recv()
            rc(*own_s(sib, sib), "v", 1, tp=sib).wait_recv()
            for o in far:
                for c in peer_copies(o, 1 - odd):
                    c.wait_recv()
            for i in range(3):
                for j in range(3):
                    wf[i, :, j * B:(j + 1) * B] = w4[i, j]
            wf[MAIN, :, W3:] = s4[...]

        def g_copy(o):
            k = owner(o)
            return rc(dzm.at[k], g0.at[tp], "g", o, stage=0, tp=k)

        def tile(img, t):
            h0 = t * HT
            acc = None
            for i in range(3):
                d = jnp.dot(x4[img, pl.ds(h0 + i, HT)].reshape(M, C), wf[i], preferred_element_type=F32)
                acc = d if acc is None else acc + d
            pre = pltpu.roll(acc[:, :B], 1, 0) + acc[:, B:2 * B] + pltpu.roll(acc[:, 2 * B:W3], M - 1, 0)
            mixed = pre * scale_main + shift_main + acc[:, W3:] * scale_short
            z = jnp.maximum(mixed, 0.0)
            for r in range(HT):
                zf[pl.ds((h0 + r) * HW * IMGS + img, HW, stride=IMGS), :] = z[r * WP:r * WP + HW]
            dz = d4[img, pl.ds(h0, HT)].reshape(M, B).astype(F32)
            dz = jnp.where(mixed > 0.0, dz, 0.0)
            dzm[img, pl.ds(h0, HT)] = dz.astype(BF).reshape(HT, WP, B)[:, :HW, :]
            g = dz * scale_main
            for j, val in enumerate((pltpu.roll(g, M - 1, 0), g, pltpu.roll(g, 1, 0), dz * scale_short)):
                g4[img, pl.ds(1 + h0, HT), :, j * B:(j + 1) * B] = val.astype(BF).reshape(HT, WP, B)

        def step(t, c):
            @pl.when(t == 0)
            def _():
                for o in far:
                    for c in far_recv(o):
                        c.wait_recv()
                    for c in peer_copies(o, odd):
                        c.start()

            for o in range(IMGS):
                k = t - o

                @pl.when(jnp.logical_and(k >= 0, k < NT))
                def _():
                    land(o, k)

            @pl.when(t == 1)
            def _():
                weights()

            def per_image(o, c2):
                img = owner(o)
                k = t - o - 1

                @pl.when(jnp.logical_and(k >= 0, k < NT))
                def _():
                    tile(img, k)

                @pl.when(k == NT - 1)
                def _():
                    @pl.when(o < 2)
                    def _():
                        g_copy(o).start()

                    xt[img] = x4[img, 1:HW + 1].reshape(HW * WP, C).T

                return c2

            return lax.fori_loop(0, IMGS, per_image, c)

        with jax.named_scope("s1_fwd"):
            lax.fori_loop(0, 2 * NT, step, 0)

        def part_near(k, q):
            return rc(part.at[k, :, pl.ds(0, W3)], pa.at[k, :, pl.ds(0, W3)], "p", k, tp=q)

        def part_main(k):
            return rc(part.at[4 * IMGS + k], pa.at[k], "q", k, stage=0)

        def weight_grad(i, n, done):
            def half_step(e, c):
                hx = jnp.where(e == 0, 1 - half, half)
                c0 = pl.multiple_of(hx * 2 * B, 2 * B)
                acc = None
                for img in range(IMGS):
                    rhs = g4[img, 2 - i:2 - i + HW, :, :n].reshape(HW * WP, n)
                    d = jnp.dot(xt[img, pl.ds(c0, 2 * B), :], rhs, preferred_element_type=F32)
                    acc = d if acc is None else acc + d
                for p in range(2):
                    for h in range(2):
                        r = p * B + h * R
                        done(e, p, h, 2 * hx + p, acc[r:r + R])
                return c

            lax.fori_loop(0, 2, half_step, 0)

        def near_chunk(e, p, h, idx):
            return 4 * idx + 4 * len(NEAR) * (1 - e) + 2 * h + lax.rem(p + par, 2)

        def near_done(idx):
            def done(e, p, h, q, val):
                k = near_chunk(e, p, h, idx)

                @pl.when(q == tp)
                def _():
                    pa[k, :, :W3] = val

                @pl.when(q != tp)
                def _():
                    part[k, :, :W3] = val
                    part_near(k, q).start()

            return done

        def main_done(e, p, h, q, val):
            k = 4 * e + 2 * h + p
            part[4 * IMGS + k] = val
            part_main(k).start()

        def p_wait(k):
            @pl.when(jnp.logical_or(k >= 4 * len(NEAR), lax.rem(k, 2) == 1))
            def _():
                part_near(k, sib).wait_recv()

        with jax.named_scope("s1_dw"):
            weight_grad(NEAR[0], W3, near_done(0))
            send_up((0, 2), W3, p_wait)
            weight_grad(MAIN, C, main_done)
            send_up((1, 3), W3, p_wait)
            weight_grad(NEAR[1], W3, near_done(1))
            send_up(range(4, 8), W3, p_wait)
            for o in far:
                g_copy(o).start()
            zb[...] = zf[...].astype(BF)
            z_copy = local(zb, z_out, 4)
            z_copy.start()

        def place(i, src, ref, k, h):
            for j in range(3):
                ob[i, j, h * R:(h + 1) * R, lanes(src)] = ref[k, :, j * B:(j + 1) * B]

        with jax.named_scope("s1_ar"):
            send_up(range(8, 16), W3, p_wait)
            all_reduce(4 * len(NEAR), W3, p_wait, lambda k: None)
        outs = [local(ob.at[i], dw_out.at[i], 5 + i) for i in range(3)]
        with jax.named_scope("s1_out"):
            for idx, i in enumerate(NEAR):
                for o in range(IMGS):
                    for h in range(2):
                        place(i, owner(o), ff, 4 * idx + 4 * len(NEAR) * (o // 2) + 2 * h + o % 2, h)
                outs[i].start()
            for h in range(2):
                for o in range(IMGS):
                    src = owner(o)
                    rc(ff.at[o], fo.at[h, src], "o", o, land=(2 * src + h,), stage=0).wait_recv()
                    place(MAIN, src, fo.at[h], src, h)
                    obs[h * R:(h + 1) * R, lanes(src)] = fo[h, src, :, W3:]
            outs[MAIN].start()
            outs.append(local(obs, ds_out, 8))
            outs[-1].start()

        for o in far:
            w_sends.extend(peer_copies(o, odd))
        for c in w_sends:
            c.wait_send()
        for c in quarters:
            c.wait_send()

        def drain(k, c):
            g_copy(k).wait_send()
            rc(rows(tp, k), rows(tp, k), "b", k, tp=sib).wait_send()
            rc(rows(nbx, k), rows(nbx, k), "d", k, tp=sib).wait_send()
            part_main(k).wait_send()
            part_main(IMGS + k).wait_send()

            @pl.when(k >= NCROSS)
            def _():
                rc(rows(tp, k), rows(tp, k), "c", k, tp=nbx).wait_send()

            return c

        lax.fori_loop(0, NT, drain, 0)
        for idx in range(len(NEAR)):
            for e in range(2):
                for p in range(2):
                    q = 2 * jnp.where(e == 0, 1 - half, half) + p

                    @pl.when(q != tp)
                    def _():
                        for h in range(2):
                            part_near(near_chunk(e, p, h, idx), q).wait_send()
        for c in (z_copy, *outs):
            c.wait()

    @pl.when(st == 0)
    def _():
        def rows(k):
            return act.at[pl.ds(k * HT, HT)], xl.at[tp, pl.ds(k * HT, HT)]

        sends = [rc(*rows(k), "a", k, stage=1) for k in range(NT)]
        sends += [rc(*rows(k), "c", k, stage=1, tp=nbx) for k in range(NCROSS)]
        for c in sends:
            c.start()

        def wref(q, k):
            return w0.at[k, :, q] if k < 3 else s0.at[q]

        def hop(name, q, k, dst):
            return rc(wref(q, k), wref(q, k), name, k, tp=dst)

        with jax.named_scope("s0_relay"):
            for k in range(NT + 1):
                if k < NT:
                    rc(wref(tp, k), wref(tp, k), "a", k, stage=1).wait_recv()
                    hop("c", tp, k, nbx).start()
                    hop("b", tp, k, sib).start()
                if k > 0:
                    hop("c", nbx, k - 1, nbx).wait_recv()
                    hop("d", nbx, k - 1, sib).start()
        edge = jnp.zeros((WP, C), BF)
        gp[0] = edge
        gp[HW + 1] = edge
        gp[:, 24:, :] = jnp.zeros((HW + 2, 8, C), BF)
        gsp[:, 24:, :] = jnp.zeros((HW, 8, C), BF)

        def p_wait(k):
            rc(pa.at[k], pa.at[k], "q", k, stage=1).wait_recv()

        def result(k):
            q = 2 * jnp.where(k < IMGS, 1 - half, half) + lax.rem(k, 2)
            h = lax.rem(k, IMGS) // 2
            return rc(ff.at[k], fo.at[h, tp], "o", k, land=(2 * tp + h,), stage=1, tp=q)

        with jax.named_scope("s0_ar"):
            send_up(range(2 * IMGS), C, p_wait)
            all_reduce(IMGS, C, p_wait, lambda k: result(k).start())

        with jax.named_scope("s0_wait"):
            for k in range(NT):
                hop("b", sib, k, sib).wait_recv()
                hop("d", dia, k, sib).wait_recv()
            for o in range(IMGS):
                q = owner(o)
                rc(gam, ga.at[q], "y", o, stage=1, tp=q).wait_recv()
                rc(gams, gsa.at[q], "u", o, stage=1, tp=q).wait_recv()
                rc(dzm.at[tp], g0.at[q], "g", o, stage=1, tp=q).wait_recv()

        def build(h, c):
            for q in range(IMGS):
                dz = g0[q, h].astype(F32)
                gp[1 + h, :HW, q * B:(q + 1) * B] = (dz * ga[q]).astype(BF)
                gsp[h, :HW, q * B:(q + 1) * B] = (dz * gsa[q]).astype(BF)
            return c

        contract = (((1,), (1,)), ((), ()))

        def dx_tile(t, c):
            h0 = t * HT
            total = None
            for j in (1, 0, 2):
                d = None
                for i in range(3):
                    lhs = gp[pl.ds(h0 + 2 - i, HT)].reshape(M, C)
                    p = lax.dot_general(lhs, w0[i, j].reshape(C, C), contract, preferred_element_type=F32)
                    d = p if d is None else d + p
                if j == 1:
                    d += lax.dot_general(gsp[pl.ds(h0, HT)].reshape(M, C), s0[...].reshape(C, C), contract, preferred_element_type=F32)
                else:
                    d = pltpu.roll(d, M - 1 if j == 0 else 1, 0)
                total = d if total is None else total + d
            dxb[pl.ds(h0, HT)] = total.astype(BF).reshape(HT, WP, C)[:, :HW, :]
            return c

        with jax.named_scope("s0_dx"):
            lax.fori_loop(0, HW, build, 0)
            lax.fori_loop(0, NT, dx_tile, 0)
        dx_copy = local(dxb, dx_out, 5)
        dx_copy.start()

        for c in sends:
            c.wait_send()
        for k in range(NT):
            hop("c", tp, k, nbx).wait_send()
            hop("b", tp, k, sib).wait_send()
            hop("d", nbx, k, sib).wait_send()
        for k in range(2 * IMGS):
            result(k).wait_send()
        dx_copy.wait()


def scratch_shapes():
    def v(*shape, dtype=BF):
        return pltpu.VMEM(shape, dtype)

    def f(*shape):
        return pltpu.VMEM(shape, F32)

    n = HW * HW * IMGS
    buffers = [
        v(IMGS, HW, HW, C),
        v(IMGS, HW + 2, WP, C),
        v(IMGS, C, HW * WP),
        v(3, 3, C, B),
        v(C, B),
        v(3, C, C),
        v(n, B),
        f(n, B),
        v(IMGS, HW, WP, B),
        v(IMGS, HW, HW, B),
        f(n, B),
        v(n, B),
        v(IMGS, HW + 2, WP, C),
        f(6 * IMGS, R, C),
        f(4 * IMGS, R, C),
        f(4 * IMGS, R, C),
        f(2 * IMGS, R, C),
        f(2 * IMGS, R, C),
        f(4 * IMGS, R, C),
        f(2, IMGS, R, C),
        f(3, 3, B, C),
        f(B, C),
        v(3, 3, IMGS, B, C),
        v(IMGS, B, C),
        f(IMGS, 1, B),
        f(IMGS, 1, B),
        v(IMGS, HW, HW, B),
        v(HW + 2, WP, C),
        v(HW, WP, C),
        v(HW, HW, C),
    ]
    sems = {}
    for names, n in (("abcdwvyugij", IMGS), ("moq", 2 * IMGS), ("efhp", 4 * IMGS)):
        for name in names:
            sems["s" + name] = n
            sems["r" + name] = n
    sems["l"] = 9
    return [*buffers, {k: pltpu.SemaphoreType.DMA((n,)) for k, n in sems.items()}]


def place_kernel(z, dx, dw, ds, z_out, dx_out, dw_out, ds_out, zb, dxb, dwb, dsb, sem_in, sem_out):
    st = lax.axis_index("stage")
    zs = (z, zb, z_out)
    xs = (dx, dxb, dx_out)
    ws = (dw, dwb, dw_out)
    ss = (ds, dsb, ds_out)

    def move(moved, zeroed):
        copies = [(pltpu.make_async_copy(a, b, sem_in.at[k]), pltpu.make_async_copy(b, c, sem_out.at[k])) for k, (a, b, c) in enumerate(moved)]
        for load, _ in copies:
            load.start()
        fills = [pltpu.make_async_copy(b, c, sem_out.at[len(moved) + k]) for k, (_, b, c) in enumerate(zeroed)]
        for (_, b, _), c in zip(zeroed, fills):
            b[...] = jnp.zeros_like(b)
            c.start()
        for load, store in copies:
            load.wait()
            store.start()
        for _, store in copies:
            store.wait()
        for c in fills:
            c.wait()

    @pl.when(st == 1)
    def _():
        move([zs, ss, ws], [xs])

    @pl.when(st == 0)
    def _():
        move([xs], [zs, ss, ws])


def solution(mesh):
    act_spec = P("stage", ("dp", "tp"), None, None, None)
    kernel_spec = P("stage", None, None, "tp", None)
    short_spec = P("stage", "tp", None)
    vec_spec = P("stage", "tp")
    grad_spec = P("stage", "dp", None, None, "tp")
    any_ = pl.BlockSpec(memory_space=pl.ANY)
    vm = pl.BlockSpec(memory_space=pltpu.VMEM)

    def device_step(act_in, w_conv, w_short, gamma, beta, gamma_s, grad_z):
        by_pixel = (0, 2, 3, 1, 4)
        grads = jnp.transpose(grad_z, by_pixel).reshape(-1, B)
        call = pl.pallas_call(
            block_kernel,
            out_shape=(
                jax.ShapeDtypeStruct(grads.shape, BF),
                jax.ShapeDtypeStruct(act_in.shape[2:], BF),
                jax.ShapeDtypeStruct(w_conv.shape[1:], F32),
                jax.ShapeDtypeStruct(w_short.shape[1:], F32),
            ),
            in_specs=[any_, any_, any_, vm, vm, vm, any_],
            out_specs=(any_, any_, any_, any_),
            scratch_shapes=scratch_shapes(),
            compiler_params=pltpu.CompilerParams(vmem_limit_bytes=64000000, has_side_effects=True),
        )
        found = call(act_in[0, 0], w_conv[0], w_short[0], gamma, beta, gamma_s, grads)
        z, dx, dw, ds = pl.pallas_call(
            place_kernel,
            out_shape=tuple(jax.ShapeDtypeStruct(a.shape, a.dtype) for a in found),
            in_specs=[any_] * 4,
            out_specs=(any_,) * 4,
            scratch_shapes=[*(pltpu.VMEM(a.shape, a.dtype) for a in found), pltpu.SemaphoreType.DMA((4,)), pltpu.SemaphoreType.DMA((4,))],
            compiler_params=pltpu.CompilerParams(vmem_limit_bytes=64000000),
        )(*found)
        z = jnp.transpose(z.reshape(1, HW, HW, IMGS, B), (0, 3, 1, 2, 4))
        return z, dx[None, None], dw[None], ds[None]

    return jax.shard_map(device_step, mesh=mesh, in_specs=(act_spec, kernel_spec, short_spec, vec_spec, vec_spec, vec_spec, grad_spec), out_specs=(grad_spec, act_spec, kernel_spec, short_spec), check_vma=False)
```

time: 432 us -> 118 us (0.27); the launches traced: 427 us -> 118 us
  waiting for transfers between devices: 251 us -> 0 us
  Pallas kernels: 0 us -> 118 us
  local copies, waits for them, and re-layouts: 84 us -> 0 us
  matrix products: 39.8 us -> 0 us
  blocking collectives: 15.9 us -> 0 us
  between operations: 14.2 us -> 0.64 us
  other arithmetic: 12.7 us -> 0 us
  starting transfers between devices: 8.65 us -> 0 us
    reduce_scatter x2 -> x0, waiting for transfers between devices: 126 us -> none  [device_step(): lax.psum_scatter((pre_part, short_part), 'tp', scatter_dimension=3, tiled...]
    pallas_call x0 -> x2, Pallas kernels: none -> 118 us  [the longest x1 115 us: device_step(): call(act_in[0, 0], w_conv[0], w_short[0], gamma, beta, gamma_s, grads)]
    psum x1 -> x0, waiting for transfers between devices: 44 us -> none  [device_step(): dw_sum, dws_sum = lax.psum((dw_part, dws_part), 'dp')]
    conv_general_dilated x8 -> x0, local copies, waits for them, and re-layouts: 38.2 us -> none  [conv_same(): lax.conv_general_dilated(left_op, right_op, (1, 1), 'SAME', dimension_num...]
    ppermute x2 -> x0, waiting for transfers between devices: 37.7 us -> none  [the longest x1 20.6 us: device_step(): returned = lax.ppermute(grad_local, 'stage', perm=[(1, 0)])]
    all_gather x2 -> x0, waiting for transfers between devices: 32.2 us -> none  [device_step(): lax.all_gather((g_main, g_short), 'tp', axis=3, tiled=True)]
    unnamed x31 -> x0, local copies, waits for them, and re-layouts: 32.1 us -> none
    conv_general_dilated x3 -> x0, matrix products: 30.7 us -> none  [the longest x2 18.9 us: conv_same(): lax.conv_general_dilated(left_op, right_op, (1, 1), 'SAME', dimension_num...]
  transfers between devices with their start and end apart: 8 -> 0, of which waited for: 8 -> 0; matrix products, arithmetic and copies ran while one was open for 14% -> 0% of each run, Pallas kernels for 0% -> 0%
where the time goes in v1:
time: 118 us
  Pallas kernels  118 us (100%)
    pallas_call x1, Pallas kernels, device_step(): call(act_in[0, 0], w_conv[0], w_short[0], gamma, beta, gamma_s, grads)  115 us
    pallas_call x1, Pallas kernels, device_step(): pl.pallas_call(place_kernel, out_shape=tuple((jax.ShapeDtypeStruct(a.shap...  2.6 us

profile of v1, /device:TPU:0, one launch (start us, length us, event | category | flops | bytes accessed | tf_op | source)
XLA Modules:
  0.0 118.1 jit_solution(305367334195768587)
XLA Ops:
  0.6 114.9 %shard_map.102 = (bf16[3136,128]{1,0:T(8,128)(2,1)}, bf16[28,28,512]{2,1,0:T(8,128)(2,1)}, f32[3,3,128,512]{3,2,1,0:T(8,128)}, f32[128,512]{1,0:T(8,128)}) custom-call(bf16[28,28,512]{2,1,0:T(8,128)(2,1)} %bitcast.13, bf16[3,3,128,512]{3,2,1,0:T(8,128)(2,1)} %bitcast.12, bf16[128,512]{1,0:T(8,128)(2,1)} %bitcast.15, f32[1,128]{1,0:T(1,128)} %gam.1, ...), custom_call_target="tpu_custom_call" | custom-call | tf_op jit(solution)/shard_map/pallas_call | solution.py:630
  115.5 2.6 %shard_map.103 = (bf16[3136,128]{1,0:T(8,128)(2,1)}, bf16[28,28,512]{2,1,0:T(8,128)(2,1)}, f32[3,3,128,512]{3,2,1,0:T(8,128)}, f32[128,512]{1,0:T(8,128)}) custom-call(bf16[3136,128]{1,0:T(8,128)(2,1)} %get-tuple-element.12.z, bf16[28,28,512]{2,1,0:T(8,128)(2,1)} %get-tuple-element.13.dx, f32[3,3,128,512]{3,2,1,0:T(8,128)} %get-tuple-element.14.dw, ...), custom_call_target="tpu_custom_call" | custom-call | tf_op jit(solution)/shard_map/pallas_call | solution.py:631

commit v2 on v1

v2 whole, which is shorter than its diff:
```python
import jax
import jax.numpy as jnp
from jax import lax
from jax.experimental import pallas as pl
from jax.experimental.pallas import tpu as pltpu
from jax.sharding import PartitionSpec as P

BF = jnp.bfloat16
F32 = jnp.float32
MESH = pl.DeviceIdType.MESH
B = 128
C = 4 * B
W3 = 3 * B
IMGS = 4
HW = 28
WP = 32
HT = 7
NT = 4
M = HT * WP
LAG = 8
LATE = 7
R = 32
NR = B // R
W_ROWS = 10 * B // 2
HB = B // 2
CROSS = 4
NEAR = (0, 2)
NEARS = 4 * NR * len(NEAR)
MAIN = 1


def lanes(k):
    return pl.ds(pl.multiple_of(k * B, B), B)


def block_kernel(act, wc, ws, gam, bet, gams, gz, z_out, dx_out, dw_out, ds_out,
                 xl, x4, xt, w4, s4, wf, dzl, wide, d4, dzm, zf, zb, g4, part, pa, re, rm, tt, ff, fo, ob, obs,
                 w0, s0, ga, gsa, g0, gp, gsp, dxb, sem):
    dp = lax.axis_index("dp")
    st = lax.axis_index("stage")
    tp = lax.axis_index("tp")
    par = lax.rem(tp, 2)
    half = tp // 2
    sib = tp + 1 - 2 * par
    nbx = lax.rem(tp + 2, IMGS)
    dia = lax.rem(sib + 2, IMGS)
    odd = lax.rem(dp, 2)
    peer = dp + 1 - 2 * odd

    barrier = pltpu.get_barrier_semaphore()

    def greet(**dev):
        pl.semaphore_signal(barrier, inc=1, device_id=dev, device_id_type=MESH)

    for mate in (sib, nbx, dia):
        greet(tp=mate)
        greet(stage=1 - st, tp=mate)
    greet(stage=1 - st)
    is_end = jnp.logical_or(dp == 0, dp == 3)
    inner = jnp.where(dp == 0, 1, 2)
    endn = jnp.where(dp == 1, 0, 3)
    midn = 3 - dp
    mates = 7

    @pl.when(is_end)
    def _():
        greet(dp=inner)
        pl.semaphore_wait(barrier, mates + 1)

    @pl.when(jnp.logical_not(is_end))
    def _():
        greet(dp=endn)
        greet(dp=midn)
        pl.semaphore_wait(barrier, mates + 2)

    def rc(src, dst, name, *k, land=None, **dev):
        ssem, rsem = sem["s" + name], sem["r" + name.replace("h", "e")]
        return pltpu.make_async_remote_copy(src_ref=src, dst_ref=dst, send_sem=ssem.at[0], recv_sem=rsem.at[land or k], device_id=dev, device_id_type=MESH)

    def sent(name, ref):
        pltpu.make_async_remote_copy(src_ref=ref, dst_ref=ref, send_sem=sem["s" + name].at[0], recv_sem=sem["re"].at[0], device_id={"tp": sib}, device_id_type=MESH).wait_send()

    def local(src, dst, k):
        return pltpu.make_async_copy(src, dst, sem["l"].at[k])

    def owner(o):
        return jnp.where(o == 0, tp, jnp.where(o == 1, sib, jnp.where(o == 2, nbx, dia)))

    def up(k, n):
        return rc(pa.at[k, :, pl.ds(0, n)], re.at[k, :, pl.ds(0, n)], "e", k, dp=inner)

    def arrive(k, n, emit):
        ref = ff.at[k, :, pl.ds(0, n)]
        rc(ref, ref, "h", k, dp=inner).wait_recv()
        emit(k)

    def send_up(ks, n, p_wait, lag=None, emit=None):
        @pl.when(is_end)
        def _():
            for k in ks:
                p_wait(k)
                up(k, n).start()
                if lag is not None and k >= lag:
                    arrive(k - lag, n, emit)

    def e_wait(k, n):
        rc(pa.at[k, :, pl.ds(0, n)], re.at[k, :, pl.ds(0, n)], "e", k, dp=endn).wait_recv()

    def to_root(m, n):
        return rc(tt.at[m, :, pl.ds(0, n)], rm.at[m, :, pl.ds(0, n)], "m", m, dp=midn)

    def pass_on(m, n, p_wait):
        k = 2 * m + 2 - dp
        p_wait(k)
        e_wait(k, n)
        tt[m, :, :n] = pa[k, :, :n] + re[k, :, :n]
        to_root(m, n).start()

    def all_reduce(pairs, n, p_wait, emit, outer_work=None, inner_work=None, first=0, ahead=1):
        def cols(ref, k):
            return ref.at[k, :, pl.ds(0, n)]

        @pl.when(is_end)
        def _():
            for k in range(first, 2 * pairs):
                if outer_work and k in outer_work:
                    outer_work[k]()
                arrive(k, n, emit)
            sent("e", pa.at[pl.ds(0, 2 * pairs), :, pl.ds(0, n)])

        @pl.when(jnp.logical_not(is_end))
        def _():
            def mine(m):
                return 2 * m + dp - 1

            def other(m):
                return 2 * m + 2 - dp

            def to_mid(k, m):
                return rc(cols(ff, k), cols(ff, k), "f", m, dp=midn)

            def to_end(k):
                return rc(cols(ff, k), cols(ff, k), "h", k, dp=endn)

            def forward_result(m):
                k = other(m)
                rc(cols(ff, k), cols(ff, k), "f", m, dp=midn).wait_recv()
                to_end(k).start()
                emit(k)

            for m in range(ahead):
                pass_on(m, n, p_wait)
            for m in range(pairs):
                if m + ahead < pairs:
                    pass_on(m + ahead, n, p_wait)
                if inner_work and m in inner_work:
                    inner_work[m]()
                k = mine(m)
                p_wait(k)
                e_wait(k, n)
                to_root(m, n).wait_recv()
                ff[k, :, :n] = pa[k, :, :n] + re[k, :, :n] + rm[m, :, :n]
                to_end(k).start()
                to_mid(k, m).start()
                emit(k)
                if m > 0:
                    forward_result(m - 1)
            forward_result(pairs - 1)
            half_of = pl.ds(0, pairs)
            sent("m", tt.at[half_of, :, pl.ds(0, n)])
            sent("f", tt.at[half_of, :, pl.ds(0, n)])
            sent("h", pa.at[pl.ds(0, 2 * pairs), :, pl.ds(0, n)])

    @pl.when(st == 1)
    def _():
        def own_w(k, dst_k):
            return wc.at[:, :, :, lanes(k)], w4.at[:, :, lanes(dst_k)]

        def own_s(k, dst_k):
            return ws.at[:, lanes(k)], s4.at[lanes(dst_k)]

        loads = [local(gz, dzl, 0), local(*own_w(tp, tp), 1), local(*own_s(tp, tp), 2)]
        for c in loads:
            c.start()

        def w_copy(o):
            return rc(*own_w(owner(o), tp), "w", o, tp=owner(o))

        def s_copy(o):
            return rc(*own_s(owner(o), tp), "v", o, tp=owner(o))

        def w_half(o, k, h):
            rows = pl.ds(k * B + h * HB, HB)
            return w4.at[:, :, rows], s4.at[rows]

        def far_copies(o):
            k = owner(o)
            mine = pl.ds(odd * HB, HB)
            dst_w, dst_s = w_half(o, tp, odd)
            return rc(wc.at[:, :, mine, lanes(k)], dst_w, "w", o, tp=k), rc(ws.at[mine, lanes(k)], dst_s, "v", o, tp=k)

        def far_recv(o):
            dst_w, dst_s = w_half(o, owner(o), odd)
            return rc(dst_w, dst_w, "w", o, tp=owner(o)), rc(dst_s, dst_s, "v", o, tp=owner(o))

        def peer_copies(o, h):
            dst_w, dst_s = w_half(o, owner(o), h)
            return rc(dst_w, dst_w, "i", o, dp=peer), rc(dst_s, dst_s, "j", o, dp=peer)

        far = (2, 3)
        w_sends = [*far_copies(2), *far_copies(3), w_copy(1), s_copy(1)]
        for c in w_sends:
            c.start()

        share = pl.ds(odd * HB, HB)
        quarters = [rc(wc.at[i, :, share], w0.at[i, :, tp, share], "a", i, stage=0) for i in range(3)]
        quarters.append(rc(ws.at[share], s0.at[tp, share], "a", 3, stage=0))
        for o in range(IMGS):
            quarters.append(rc(gam, ga.at[tp], "y", 0, stage=0, tp=owner(o)))
            quarters.append(rc(gams, gsa.at[tp], "u", 0, stage=0, tp=owner(o)))
        for c in quarters:
            c.start()

        edge = jnp.zeros((WP, C), BF)
        for o in range(IMGS):
            for r in (0, HW + 1):
                x4[o, r] = edge
                g4[o, r] = edge
        x4[:, :, 24:, :] = jnp.zeros((IMGS, HW + 2, 8, C), BF)
        d4[:, :, 24:, :] = jnp.zeros((IMGS, HW, 8, B), BF)
        for i in NEAR:
            wf[i, :, W3:] = jnp.zeros((C, B), BF)

        loads[0].wait()
        wide[...] = dzl[...].astype(F32)

        def split_rows(h, c):
            for o in range(IMGS):
                d4[o, h, :HW, :] = wide[pl.ds(h * HW * IMGS + o, HW, stride=IMGS), :].astype(BF)
            return c

        lax.fori_loop(0, HW, split_rows, 0)

        scale_main = gam[...]
        shift_main = bet[...]
        scale_short = gams[...]

        def rows(img, k):
            return xl.at[img, pl.ds(k * HT, HT)]

        def tail_copy(img, k):
            ref = xl.at[img, pl.ds((NT - 1) * HT + CROSS, HT - CROSS)] if k is None else rows(img, k)
            return rc(ref, ref, "c", NT - 1 if k is None else k, tp=nbx)

        def head_copy(img):
            ref = xl.at[img, pl.ds((NT - 1) * HT, CROSS)]
            return rc(ref, ref, "x", 0, stage=0)

        def each_tail(img, k, act):
            @pl.when(k < NT - 1)
            def _():
                act(tail_copy(img, k))

            @pl.when(k == NT - 1)
            def _():
                act(tail_copy(img, None))

        def land(o, k):
            img = owner(o)
            ref = rows(img, k)
            if o == 0:
                rc(ref, ref, "a", k, stage=0).wait_recv()
                rc(ref, ref, "b", k, tp=sib).start()
                each_tail(img, k, lambda c: c.start())
            elif o == 1:
                rc(ref, ref, "b", k, tp=sib).wait_recv()
            elif o == 2:
                each_tail(img, k, lambda c: c.wait_recv())

                @pl.when(k == NT - 1)
                def _():
                    head_copy(img).wait_recv()

                rc(ref, ref, "d", k, tp=sib).start()
            else:
                rc(ref, ref, "d", k, tp=sib).wait_recv()
            for r in range(HT):
                h = k * HT + r
                x4[img, 1 + h, :HW, :] = xl[img, h]

        def weights():
            for c in loads[1:]:
                c.wait()
            rc(*own_w(sib, sib), "w", 1, tp=sib).wait_recv()
            rc(*own_s(sib, sib), "v", 1, tp=sib).wait_recv()
            for o in far:
                for c in peer_copies(o, 1 - odd):
                    c.wait_recv()
            for i in range(3):
                for j in range(3):
                    wf[i, :, j * B:(j + 1) * B] = w4[i, j]
            wf[MAIN, :, W3:] = s4[...]

        def g_copy(o):
            k = owner(o)
            return rc(dzm.at[k], g0.at[tp], "g", o, stage=0, tp=k)

        def tile(img, t):
            h0 = t * HT
            acc = None
            for i in range(3):
                d = jnp.dot(x4[img, pl.ds(h0 + i, HT)].reshape(M, C), wf[i], preferred_element_type=F32)
                acc = d if acc is None else acc + d
            pre = pltpu.roll(acc[:, :B], 1, 0) + acc[:, B:2 * B] + pltpu.roll(acc[:, 2 * B:W3], M - 1, 0)
            mixed = pre * scale_main + shift_main + acc[:, W3:] * scale_short
            z = jnp.maximum(mixed, 0.0)
            for r in range(HT):
                zf[pl.ds((h0 + r) * HW * IMGS + img, HW, stride=IMGS), :] = z[r * WP:r * WP + HW]
            dz = d4[img, pl.ds(h0, HT)].reshape(M, B).astype(F32)
            dz = jnp.where(mixed > 0.0, dz, 0.0)
            dzm[img, pl.ds(h0, HT)] = dz.astype(BF).reshape(HT, WP, B)[:, :HW, :]
            g = dz * scale_main
            for j, val in enumerate((pltpu.roll(g, M - 1, 0), g, pltpu.roll(g, 1, 0), dz * scale_short)):
                g4[img, pl.ds(1 + h0, HT), :, j * B:(j + 1) * B] = val.astype(BF).reshape(HT, WP, B)

        def weight_grad(i, n, e, done):
            hx = jnp.where(e == 0, 1 - half, half)
            c0 = pl.multiple_of(hx * 2 * B, 2 * B)
            acc = None
            for img in range(IMGS):
                rhs = g4[img, 2 - i:2 - i + HW, :, :n].reshape(HW * WP, n)
                d = jnp.dot(xt[img, pl.ds(c0, 2 * B), :], rhs, preferred_element_type=F32)
                acc = d if acc is None else acc + d
            for h in range(NR):
                for p in range(2):
                    r = p * B + h * R
                    done(e, p, h, 2 * hx + p, acc[r:r + R])

        def arrived(o, k):
            img = owner(o)
            land(o, k)

            def run(t, c):
                tile(img, t)
                return c

            lax.fori_loop(jnp.maximum(k - 1, 0), jnp.where(k == NT - 1, NT, k), run, 0)

            @pl.when(k == NT - 1)
            def _():
                if o < 2:
                    g_copy(o).start()
                xt[img] = x4[img, 1:HW + 1].reshape(HW * WP, C).T

        with jax.named_scope("s1_fwd"):
            for o in far:
                for w in far_recv(o):
                    w.wait_recv()
                for w in peer_copies(o, odd):
                    w.start()
            land(0, 0)
            land(1, 0)

            def step(t, c):
                @pl.when(t == 1)
                def _():
                    weights()

                @pl.when(t < NT)
                def _():
                    for o in (0, 1):
                        arrived(o, t)

                for o in far:
                    arrived(o, t - 1)
                return c

            lax.fori_loop(1, NT + 1, step, 0)

        def part_near(k, q):
            return rc(part.at[k, :, pl.ds(0, W3)], pa.at[k, :, pl.ds(0, W3)], "p", k, tp=q)

        def part_main(k):
            return rc(part.at[NEARS + k], pa.at[k], "q", k, stage=0)

        def near_chunk(e, p, h, idx):
            return 2 * NR * (idx + len(NEAR) * (1 - e)) + 2 * h + lax.rem(p + par, 2)

        def near_done(idx):
            def done(e, p, h, q, val):
                k = near_chunk(e, p, h, idx)

                @pl.when(q == tp)
                def _():
                    pa[k, :, :W3] = val

                @pl.when(q != tp)
                def _():
                    part[k, :, :W3] = val
                    part_near(k, q).start()

            return done

        def main_done(e, p, h, q, val):
            k = 2 * NR * e + 2 * h + p
            part[NEARS + k] = val
            part_main(k).start()

        def far_grad(idx):
            weight_grad(NEAR[idx], W3, 0, near_done(idx))

        def p_wait(k):
            @pl.when(jnp.logical_or(k >= 2 * NR * len(NEAR), lax.rem(k, 2) == 1))
            def _():
                part_near(k, sib).wait_recv()

        with jax.named_scope("s1_dw"):
            weight_grad(NEAR[0], W3, 1, near_done(0))
            send_up(range(0, 2 * NR, 2), W3, p_wait)
            weight_grad(MAIN, C, 0, main_done)
            send_up(range(1, 2 * NR, 2), W3, p_wait)
            weight_grad(MAIN, C, 1, main_done)
            weight_grad(NEAR[1], W3, 1, near_done(1))

            @pl.when(is_end)
            def _():
                far_grad(0)

            send_up(range(2 * NR, 4 * NR), W3, p_wait)

            @pl.when(is_end)
            def _():
                far_grad(1)

        def place(i, src, ref, k, h):
            for j in range(3):
                ob[i, j, h * R:(h + 1) * R, lanes(src)] = ref[k, :, j * B:(j + 1) * B]

        with jax.named_scope("s1_ar"):
            send_up(range(4 * NR, NEARS), W3, p_wait)

            z_copy = local(zb, z_out, 4)

            def rest():
                for o in far:
                    g_copy(o).start()
                zb[...] = zf[...].astype(BF)
                z_copy.start()

            inner_work = {1: lambda: far_grad(0), 3: lambda: far_grad(1), LATE: rest}
            all_reduce(NEARS // 2, W3, p_wait, lambda k: None, {LATE: rest}, inner_work, ahead=3)
        outs = [local(ob.at[i], dw_out.at[i], 5 + i) for i in range(3)]
        with jax.named_scope("s1_out"):
            for idx, i in enumerate(NEAR):
                for o in range(IMGS):
                    for h in range(NR):
                        place(i, owner(o), ff, 2 * NR * (idx + len(NEAR) * (o // 2)) + 2 * h + o % 2, h)
                outs[i].start()
            for h in range(NR):
                for o in range(IMGS):
                    src = owner(o)
                    rc(ff.at[o], fo.at[h, src], "o", o, land=(NR * src + h,), stage=0).wait_recv()
                    place(MAIN, src, fo.at[h], src, h)
                    obs[h * R:(h + 1) * R, lanes(src)] = fo[h, src, :, W3:]
            outs[MAIN].start()
            outs.append(local(obs, ds_out, 8))
            outs[-1].start()

        sent("w", w4.at[:, :, pl.ds(0, 2 * B)])
        sent("v", s4.at[pl.ds(0, 2 * B)])
        sent("i", w4.at[:, :, pl.ds(0, B)])
        sent("j", s4.at[pl.ds(0, B)])
        sent("a", x4.at[0, pl.ds(0, W_ROWS // WP)])
        sent("y", ga)
        sent("u", gsa)
        sent("g", dzm)
        sent("b", xl.at[0])
        sent("c", xl.at[0, pl.ds(0, HW - CROSS)])
        sent("d", xl.at[0])
        sent("q", part.at[pl.ds(0, 4 * NR)])
        sent("p", part.at[pl.ds(0, NEARS - 2 * NR), :, pl.ds(0, W3)])
        for c in (z_copy, *outs):
            c.wait()

    @pl.when(st == 0)
    def _():
        def rows(k):
            return act.at[pl.ds(k * HT, HT)], xl.at[tp, pl.ds(k * HT, HT)]

        head = pl.ds((NT - 1) * HT, CROSS)
        sends = [rc(*rows(k), "a", k, stage=1) for k in range(NT)]
        sends.append(rc(act.at[head], xl.at[tp, head], "x", 0, stage=1, tp=nbx))
        for c in sends:
            c.start()

        def wref(q, k, part):
            rows = pl.ds(part * HB, HB)
            return w0.at[k, :, q, rows] if k < 3 else s0.at[q, rows]

        def direct(k):
            ref = wref(tp, k, odd)
            return rc(ref, ref, "a", k, stage=1)

        def across(k, part):
            ref = wref(tp, k, part)
            return rc(ref, ref, "i", k, dp=peer)

        def hop(name, q, k, second, dst):
            ref = wref(q, k, 1 - odd if second else odd)
            return rc(ref, ref, name, k + NT * second, tp=dst)

        steps = [(k, second) for k in range(NT) for second in (0, 1)]
        with jax.named_scope("s0_relay"):
            for n, (k, second) in enumerate(steps):
                if second:
                    across(k, 1 - odd).wait_recv()
                else:
                    direct(k).wait_recv()
                    across(k, odd).start()
                hop("c", tp, k, second, nbx).start()
                hop("b", tp, k, second, sib).start()
                if n > 1:
                    hop("c", nbx, *steps[n - 2], nbx).wait_recv()
                    hop("d", nbx, *steps[n - 2], sib).start()
            for back in steps[-2:]:
                hop("c", nbx, *back, nbx).wait_recv()
                hop("d", nbx, *back, sib).start()
        edge = jnp.zeros((WP, C), BF)
        gp[0] = edge
        gp[HW + 1] = edge
        gp[:, 24:, :] = jnp.zeros((HW + 2, 8, C), BF)
        gsp[:, 24:, :] = jnp.zeros((HW, 8, C), BF)

        def p_wait(k):
            rc(pa.at[k], pa.at[k], "q", k, stage=1).wait_recv()

        def result(k):
            q = 2 * jnp.where(k < 2 * NR, 1 - half, half) + lax.rem(k, 2)
            h = lax.rem(k, 2 * NR) // 2
            return rc(ff.at[k], fo.at[h, tp], "o", k, land=(NR * tp + h,), stage=1, tp=q)

        with jax.named_scope("s0_ar"):
            send_up(range(4 * NR), C, p_wait, LAG, lambda k: result(k).start())
            all_reduce(2 * NR, C, p_wait, lambda k: result(k).start(), first=4 * NR - LAG)

        with jax.named_scope("s0_wait"):
            for step in steps:
                hop("b", sib, *step, sib).wait_recv()
                hop("d", dia, *step, sib).wait_recv()
            rc(ga, ga, "y", 0, stage=1).wait_recv()
            rc(gsa, gsa, "u", 0, stage=1).wait_recv()
            for o in range(IMGS):
                q = owner(o)
                rc(dzm.at[tp], g0.at[q], "g", o, stage=1, tp=q).wait_recv()

        def build(h, c):
            for q in range(IMGS):
                dz = g0[q, h].astype(F32)
                gp[1 + h, :HW, q * B:(q + 1) * B] = (dz * ga[q]).astype(BF)
                gsp[h, :HW, q * B:(q + 1) * B] = (dz * gsa[q]).astype(BF)
            return c

        contract = (((1,), (1,)), ((), ()))

        def dx_tile(t, c):
            h0 = t * HT
            total = None
            for j in (1, 0, 2):
                d = None
                for i in range(3):
                    lhs = gp[pl.ds(h0 + 2 - i, HT)].reshape(M, C)
                    p = lax.dot_general(lhs, w0[i, j].reshape(C, C), contract, preferred_element_type=F32)
                    d = p if d is None else d + p
                if j == 1:
                    d += lax.dot_general(gsp[pl.ds(h0, HT)].reshape(M, C), s0[...].reshape(C, C), contract, preferred_element_type=F32)
                else:
                    d = pltpu.roll(d, M - 1 if j == 0 else 1, 0)
                total = d if total is None else total + d
            dxb[pl.ds(h0, HT)] = total.astype(BF).reshape(HT, WP, C)[:, :HW, :]
            return c

        with jax.named_scope("s0_dx"):
            lax.fori_loop(0, HW, build, 0)
            lax.fori_loop(0, NT, dx_tile, 0)
        dx_copy = local(dxb, dx_out, 5)
        dx_copy.start()

        sent("a", xl.at[0])
        sent("x", xl.at[0, pl.ds(0, CROSS)])
        sent("i", x4.at[0, pl.ds(0, W_ROWS // WP)])
        for name in "bcd":
            sent(name, x4.at[pl.ds(0, 2), pl.ds(0, W_ROWS // WP)])
        sent("o", ff.at[pl.ds(0, 4 * NR)])
        dx_copy.wait()


def scratch_shapes():
    def v(*shape, dtype=BF):
        return pltpu.VMEM(shape, dtype)

    def f(*shape):
        return pltpu.VMEM(shape, F32)

    n = HW * HW * IMGS
    buffers = [
        v(IMGS, HW, HW, C),
        v(IMGS, HW + 2, WP, C),
        v(IMGS, C, HW * WP),
        v(3, 3, C, B),
        v(C, B),
        v(3, C, C),
        v(n, B),
        f(n, B),
        v(IMGS, HW, WP, B),
        v(IMGS, HW, HW, B),
        f(n, B),
        v(n, B),
        v(IMGS, HW + 2, WP, C),
        f(NEARS + 4 * NR, R, C),
        f(NEARS, R, C),
        f(NEARS, R, C),
        f(NEARS // 2, R, C),
        f(NEARS // 2, R, C),
        f(NEARS, R, C),
        f(NR, IMGS, R, C),
        f(3, 3, B, C),
        f(B, C),
        v(3, 3, IMGS, B, C),
        v(IMGS, B, C),
        f(IMGS, 1, B),
        f(IMGS, 1, B),
        v(IMGS, HW, HW, B),
        v(HW + 2, WP, C),
        v(HW, WP, C),
        v(HW, HW, C),
    ]
    sems = {}
    for names, n in (("yux", 1), ("awvgij", IMGS), ("bcd", 2 * IMGS), ("oq", 4 * NR), ("mf", NEARS // 2), ("ep", NEARS)):
        for name in names:
            sems["s" + name] = 1
            sems["r" + name] = n
    sems["sh"] = 1
    sems["l"] = 9
    return [*buffers, {k: pltpu.SemaphoreType.DMA((n,)) for k, n in sems.items()}]


def place_kernel(z, dx, dw, ds, z_out, dx_out, dw_out, ds_out, zb, dxb, dwb, dsb, sem_in, sem_out):
    st = lax.axis_index("stage")
    zs = (z, zb, z_out)
    xs = (dx, dxb, dx_out)
    ws = (dw, dwb, dw_out)
    ss = (ds, dsb, ds_out)

    def move(moved, zeroed):
        copies = [(pltpu.make_async_copy(a, b, sem_in.at[k]), pltpu.make_async_copy(b, c, sem_out.at[k])) for k, (a, b, c) in enumerate(moved)]
        for load, _ in copies:
            load.start()
        fills = [pltpu.make_async_copy(b, c, sem_out.at[len(moved) + k]) for k, (_, b, c) in enumerate(zeroed)]
        for (_, b, _), c in zip(zeroed, fills):
            b[...] = jnp.zeros_like(b)
            c.start()
        for load, store in copies:
            load.wait()
            store.start()
        for _, store in copies:
            store.wait()
        for c in fills:
            c.wait()

    @pl.when(st == 1)
    def _():
        move([zs, ss, ws], [xs])

    @pl.when(st == 0)
    def _():
        move([xs], [zs, ss, ws])


def solution(mesh):
    act_spec = P("stage", ("dp", "tp"), None, None, None)
    kernel_spec = P("stage", None, None, "tp", None)
    short_spec = P("stage", "tp", None)
    vec_spec = P("stage", "tp")
    grad_spec = P("stage", "dp", None, None, "tp")
    any_ = pl.BlockSpec(memory_space=pl.ANY)
    vm = pl.BlockSpec(memory_space=pltpu.VMEM)

    def device_step(act_in, w_conv, w_short, gamma, beta, gamma_s, grad_z):
        by_pixel = (0, 2, 3, 1, 4)
        grads = jnp.transpose(grad_z, by_pixel).reshape(-1, B)
        call = pl.pallas_call(
            block_kernel,
            out_shape=(
                jax.ShapeDtypeStruct(grads.shape, BF),
                jax.ShapeDtypeStruct(act_in.shape[2:], BF),
                jax.ShapeDtypeStruct(w_conv.shape[1:], F32),
                jax.ShapeDtypeStruct(w_short.shape[1:], F32),
            ),
            in_specs=[any_, any_, any_, vm, vm, vm, any_],
            out_specs=(any_, any_, any_, any_),
            scratch_shapes=scratch_shapes(),
            compiler_params=pltpu.CompilerParams(vmem_limit_bytes=64000000, has_side_effects=True, collective_id=0),
        )
        found = call(act_in[0, 0], w_conv[0], w_short[0], gamma, beta, gamma_s, grads)
        z, dx, dw, ds = pl.pallas_call(
            place_kernel,
            out_shape=tuple(jax.ShapeDtypeStruct(a.shape, a.dtype) for a in found),
            in_specs=[any_] * 4,
            out_specs=(any_,) * 4,
            scratch_shapes=[*(pltpu.VMEM(a.shape, a.dtype) for a in found), pltpu.SemaphoreType.DMA((4,)), pltpu.SemaphoreType.DMA((4,))],
            compiler_params=pltpu.CompilerParams(vmem_limit_bytes=64000000),
        )(*found)
        z = jnp.transpose(z.reshape(1, HW, HW, IMGS, B), (0, 3, 1, 2, 4))
        return z, dx[None, None], dw[None], ds[None]

    return jax.shard_map(device_step, mesh=mesh, in_specs=(act_spec, kernel_spec, short_spec, vec_spec, vec_spec, vec_spec, grad_spec), out_specs=(grad_spec, act_spec, kernel_spec, short_spec), check_vma=False)
```

time: 118 us -> 94.4 us (0.80)
  Pallas kernels: 118 us -> 93.4 us
    pallas_call x1, Pallas kernels: 115 us -> 90.8 us  [device_step(): call(act_in[0, 0], w_conv[0], w_short[0], gamma, beta, gamma_s, grads)]
where the time goes in v2:
time: 94.4 us; the launch traced here: 94.2 us
  Pallas kernels  93.4 us (99%)
    pallas_call x1, Pallas kernels, device_step(): call(act_in[0, 0], w_conv[0], w_short[0], gamma, beta, gamma_s, grads)  90.8 us
    pallas_call x1, Pallas kernels, device_step(): pl.pallas_call(place_kernel, out_shape=tuple((jax.ShapeDtypeStruct(a.shap...  2.6 us

profile of v2, /device:TPU:0, one launch (start us, length us, event | category | flops | bytes accessed | tf_op | source)
XLA Modules:
  0.0 94.2 jit_solution(17732933117099772618)
XLA Ops:
  0.6 90.8 %shard_map.102 = (bf16[3136,128]{1,0:T(8,128)(2,1)}, bf16[28,28,512]{2,1,0:T(8,128)(2,1)}, f32[3,3,128,512]{3,2,1,0:T(8,128)}, f32[128,512]{1,0:T(8,128)}) custom-call(bf16[28,28,512]{2,1,0:T(8,128)(2,1)} %bitcast.13, bf16[3,3,128,512]{3,2,1,0:T(8,128)(2,1)} %bitcast.12, bf16[128,512]{1,0:T(8,128)(2,1)} %bitcast.15, f32[1,128]{1,0:T(1,128)} %gam.1, ...), custom_call_target="tpu_custom_call" | custom-call | tf_op jit(solution)/shard_map/pallas_call | solution.py:704
  91.4 2.6 %shard_map.103 = (bf16[3136,128]{1,0:T(8,128)(2,1)}, bf16[28,28,512]{2,1,0:T(8,128)(2,1)}, f32[3,3,128,512]{3,2,1,0:T(8,128)}, f32[128,512]{1,0:T(8,128)}) custom-call(bf16[3136,128]{1,0:T(8,128)(2,1)} %get-tuple-element.12.z, bf16[28,28,512]{2,1,0:T(8,128)(2,1)} %get-tuple-element.13.dx, f32[3,3,128,512]{3,2,1,0:T(8,128)} %get-tuple-element.14.dw, ...), custom_call_target="tpu_custom_call" | custom-call | tf_op jit(solution)/shard_map/pallas_call | solution.py:705

commit v3 on v2

--- a/solution.py
+++ b/solution.py
@@ -17,7 +17,9 @@
 HT = 7
 NT = 4
 M = HT * WP
-LAG = 8
+BIG_VMEM = 56000000
+SMALL_VMEM = 12000000
+LAG = 12
 LATE = 7
 R = 32
 NR = B // R
@@ -34,8 +36,8 @@
 
 
 def block_kernel(act, wc, ws, gam, bet, gams, gz, z_out, dx_out, dw_out, ds_out,
-                 xl, x4, xt, w4, s4, wf, dzl, wide, d4, dzm, zf, zb, g4, part, pa, re, rm, tt, ff, fo, ob, obs,
-                 w0, s0, ga, gsa, g0, gp, gsp, dxb, sem):
+                 xl, x4, xt, w4, s4, wf, dzl, wide, d4, dzm, zf, g4, part, pa, re, rm, tt, ff, fo,
+                 w0, s0, ga, gsa, g0, gp, gsp, sem):
     dp = lax.axis_index("dp")
     st = lax.axis_index("stage")
     tp = lax.axis_index("tp")
@@ -342,14 +344,15 @@
 
             def run(t, c):
                 tile(img, t)
+                if o < 2:
+                    some = pl.ds(t * HT, HT)
+                    rc(dzm.at[img, some], g0.at[tp, some], "g", o, stage=0, tp=img).start()
                 return c
 
             lax.fori_loop(jnp.maximum(k - 1, 0), jnp.where(k == NT - 1, NT, k), run, 0)
 
             @pl.when(k == NT - 1)
             def _():
-                if o < 2:
-                    g_copy(o).start()
                 xt[img] = x4[img, 1:HW + 1].reshape(HW * WP, C).T
 
         with jax.named_scope("s1_fwd"):
@@ -434,37 +437,29 @@
 
         def place(i, src, ref, k, h):
             for j in range(3):
-                ob[i, j, h * R:(h + 1) * R, lanes(src)] = ref[k, :, j * B:(j + 1) * B]
+                dw_out[i, j, h * R:(h + 1) * R, lanes(src)] = ref[k, :, j * B:(j + 1) * B]
 
         with jax.named_scope("s1_ar"):
             send_up(range(4 * NR, NEARS), W3, p_wait)
-
-            z_copy = local(zb, z_out, 4)
 
             def rest():
                 for o in far:
                     g_copy(o).start()
-                zb[...] = zf[...].astype(BF)
-                z_copy.start()
+                z_out[...] = zf[...].astype(BF)
 
             inner_work = {1: lambda: far_grad(0), 3: lambda: far_grad(1), LATE: rest}
-            all_reduce(NEARS // 2, W3, p_wait, lambda k: None, {LATE: rest}, inner_work, ahead=3)
-        outs = [local(ob.at[i], dw_out.at[i], 5 + i) for i in range(3)]
+            all_reduce(NEARS // 2, W3, p_wait, lambda k: None, {LATE: rest}, inner_work, ahead=2)
         with jax.named_scope("s1_out"):
             for idx, i in enumerate(NEAR):
                 for o in range(IMGS):
                     for h in range(NR):
                         place(i, owner(o), ff, 2 * NR * (idx + len(NEAR) * (o // 2)) + 2 * h + o % 2, h)
-                outs[i].start()
             for h in range(NR):
                 for o in range(IMGS):
                     src = owner(o)
                     rc(ff.at[o], fo.at[h, src], "o", o, land=(NR * src + h,), stage=0).wait_recv()
                     place(MAIN, src, fo.at[h], src, h)
-                    obs[h * R:(h + 1) * R, lanes(src)] = fo[h, src, :, W3:]
-            outs[MAIN].start()
-            outs.append(local(obs, ds_out, 8))
-            outs[-1].start()
+                    ds_out[h * R:(h + 1) * R, lanes(src)] = fo[h, src, :, W3:]
 
         sent("w", w4.at[:, :, pl.ds(0, 2 * B)])
         sent("v", s4.at[pl.ds(0, 2 * B)])
@@ -479,8 +474,6 @@
         sent("d", xl.at[0])
         sent("q", part.at[pl.ds(0, 4 * NR)])
         sent("p", part.at[pl.ds(0, NEARS - 2 * NR), :, pl.ds(0, W3)])
-        for c in (z_copy, *outs):
-            c.wait()
 
     @pl.when(st == 0)
     def _():
@@ -576,14 +569,12 @@
                 else:
                     d = pltpu.roll(d, M - 1 if j == 0 else 1, 0)
                 total = d if total is None else total + d
-            dxb[pl.ds(h0, HT)] = total.astype(BF).reshape(HT, WP, C)[:, :HW, :]
+            dx_out[pl.ds(h0, HT)] = total.astype(BF).reshape(HT, WP, C)[:, :HW, :]
             return c
 
         with jax.named_scope("s0_dx"):
             lax.fori_loop(0, HW, build, 0)
             lax.fori_loop(0, NT, dx_tile, 0)
-        dx_copy = local(dxb, dx_out, 5)
-        dx_copy.start()
 
         sent("a", xl.at[0])
         sent("x", xl.at[0, pl.ds(0, CROSS)])
@@ -591,7 +582,6 @@
         for name in "bcd":
             sent(name, x4.at[pl.ds(0, 2), pl.ds(0, W_ROWS // WP)])
         sent("o", ff.at[pl.ds(0, 4 * NR)])
-        dx_copy.wait()
 
 
 def scratch_shapes():
@@ -614,7 +604,6 @@
         v(IMGS, HW, WP, B),
         v(IMGS, HW, HW, B),
         f(n, B),
-        v(n, B),
         v(IMGS, HW + 2, WP, C),
         f(NEARS + 4 * NR, R, C),
         f(NEARS, R, C),
@@ -623,8 +612,6 @@
         f(NEARS // 2, R, C),
         f(NEARS, R, C),
         f(NR, IMGS, R, C),
-        f(3, 3, B, C),
-        f(B, C),
         v(3, 3, IMGS, B, C),
         v(IMGS, B, C),
         f(IMGS, 1, B),
@@ -632,7 +619,6 @@
         v(IMGS, HW, HW, B),
         v(HW + 2, WP, C),
         v(HW, WP, C),
-        v(HW, HW, C),
     ]
     sems = {}
     for names, n in (("yux", 1), ("awvgij", IMGS), ("bcd", 2 * IMGS), ("oq", 4 * NR), ("mf", NEARS // 2), ("ep", NEARS)):
@@ -640,40 +626,38 @@
             sems["s" + name] = 1
             sems["r" + name] = n
     sems["sh"] = 1
-    sems["l"] = 9
+    sems["l"] = 3
     return [*buffers, {k: pltpu.SemaphoreType.DMA((n,)) for k, n in sems.items()}]
 
 
-def place_kernel(z, dx, dw, ds, z_out, dx_out, dw_out, ds_out, zb, dxb, dwb, dsb, sem_in, sem_out):
+def place_kernel(z, dx, dw, ds, z_out, dx_out, dw_out, ds_out, zb, dxb, dwb, dsb, sem):
     st = lax.axis_index("stage")
-    zs = (z, zb, z_out)
-    xs = (dx, dxb, dx_out)
-    ws = (dw, dwb, dw_out)
-    ss = (ds, dsb, ds_out)
-
-    def move(moved, zeroed):
-        copies = [(pltpu.make_async_copy(a, b, sem_in.at[k]), pltpu.make_async_copy(b, c, sem_out.at[k])) for k, (a, b, c) in enumerate(moved)]
-        for load, _ in copies:
-            load.start()
-        fills = [pltpu.make_async_copy(b, c, sem_out.at[len(moved) + k]) for k, (_, b, c) in enumerate(zeroed)]
-        for (_, b, _), c in zip(zeroed, fills):
-            b[...] = jnp.zeros_like(b)
+
+    def move(*pairs):
+        copies = [pltpu.make_async_copy(a, b, sem.at[k]) for k, (a, b) in enumerate(pairs)]
+        for c in copies:
             c.start()
-        for load, store in copies:
-            load.wait()
-            store.start()
-        for _, store in copies:
-            store.wait()
-        for c in fills:
-            c.wait()
+        return copies
 
     @pl.when(st == 1)
     def _():
-        move([zs, ss, ws], [xs])
+        copies = move((dw, dw_out), (ds, ds_out), (z, z_out))
+        dxb[...] = jnp.zeros_like(dxb)
+        fill = pltpu.make_async_copy(dxb, dx_out, sem.at[3])
+        fill.start()
+        for c in (*copies, fill):
+            c.wait()
 
     @pl.when(st == 0)
     def _():
-        move([xs], [zs, ss, ws])
+        copies = move((dx, dx_out))
+        for b in (zb, dwb, dsb):
+            b[...] = jnp.zeros_like(b)
+        fills = [pltpu.make_async_copy(b, c, sem.at[1 + k]) for k, (b, c) in enumerate(((zb, z_out), (dwb, dw_out), (dsb, ds_out)))]
+        for c in fills:
+            c.start()
+        for c in (*copies, *fills):
+            c.wait()
 
 
 def solution(mesh):
@@ -691,24 +675,24 @@
         call = pl.pallas_call(
             block_kernel,
             out_shape=(
-                jax.ShapeDtypeStruct(grads.shape, BF),
-                jax.ShapeDtypeStruct(act_in.shape[2:], BF),
-                jax.ShapeDtypeStruct(w_conv.shape[1:], F32),
-                jax.ShapeDtypeStruct(w_short.shape[1:], F32),
+                pltpu.VMEM(grads.shape, BF),
+                pltpu.VMEM(act_in.shape[2:], BF),
+                pltpu.VMEM(w_conv.shape[1:], F32),
+                pltpu.VMEM(w_short.shape[1:], F32),
             ),
             in_specs=[any_, any_, any_, vm, vm, vm, any_],
-            out_specs=(any_, any_, any_, any_),
+            out_specs=(vm,) * 4,
             scratch_shapes=scratch_shapes(),
-            compiler_params=pltpu.CompilerParams(vmem_limit_bytes=64000000, has_side_effects=True, collective_id=0),
+            compiler_params=pltpu.CompilerParams(vmem_limit_bytes=BIG_VMEM, has_side_effects=True, collective_id=0),
         )
         found = call(act_in[0, 0], w_conv[0], w_short[0], gamma, beta, gamma_s, grads)
         z, dx, dw, ds = pl.pallas_call(
             place_kernel,
             out_shape=tuple(jax.ShapeDtypeStruct(a.shape, a.dtype) for a in found),
-            in_specs=[any_] * 4,
+            in_specs=[vm] * 4,
             out_specs=(any_,) * 4,
-            scratch_shapes=[*(pltpu.VMEM(a.shape, a.dtype) for a in found), pltpu.SemaphoreType.DMA((4,)), pltpu.SemaphoreType.DMA((4,))],
-            compiler_params=pltpu.CompilerParams(vmem_limit_bytes=64000000),
+            scratch_shapes=[*(pltpu.VMEM(a.shape, a.dtype) for a in found), pltpu.SemaphoreType.DMA((4,))],
+            compiler_params=pltpu.CompilerParams(vmem_limit_bytes=SMALL_VMEM),
         )(*found)
         z = jnp.transpose(z.reshape(1, HW, HW, IMGS, B), (0, 3, 1, 2, 4))
         return z, dx[None, None], dw[None], ds[None]

time: 94.4 us -> 89.6 us (0.949)
  Pallas kernels: 93.4 us -> 88.4 us
    pallas_call x1, Pallas kernels: 90.8 us -> 86.3 us  [device_step(): call(act_in[0, 0], w_conv[0], w_short[0], gamma, beta, gamma_s, grads)]
where the time goes in v3:
time: 89.6 us; the launch traced here: 89.2 us
  Pallas kernels  88.4 us (99%)
    pallas_call x1, Pallas kernels, device_step(): call(act_in[0, 0], w_conv[0], w_short[0], gamma, beta, gamma_s, grads)  86.3 us
    pallas_call x1, Pallas kernels, device_step(): pl.pallas_call(place_kernel, out_shape=tuple((jax.ShapeDtypeStruct(a.shap...  2.1 us

profile of v3, /device:TPU:0, one launch (start us, length us, event | category | flops | bytes accessed | tf_op | source)
XLA Modules:
  0.0 89.2 jit_solution(8342985445972354445)
XLA Ops:
  0.6 86.3 %shard_map.102 = (bf16[3136,128]{1,0:T(8,128)(2,1)S(1)}, bf16[28,28,512]{2,1,0:T(8,128)(2,1)S(1)}, f32[3,3,128,512]{3,2,1,0:T(8,128)S(1)}, f32[128,512]{1,0:T(8,128)S(1)}) custom-call(bf16[28,28,512]{2,1,0:T(8,128)(2,1)} %bitcast.13, bf16[3,3,128,512]{3,2,1,0:T(8,128)(2,1)} %bitcast.12, bf16[128,512]{1,0:T(8,128)(2,1)} %bitcast.15, f32[1,128]{1,0:T(1,128)} %gam.1, ...), custom_call_target="tpu_custom_call" | custom-call | tf_op jit(solution)/shard_map/pallas_call | solution.py:688
  87.0 2.1 %shard_map.103 = (bf16[3136,128]{1,0:T(8,128)(2,1)}, bf16[28,28,512]{2,1,0:T(8,128)(2,1)}, f32[3,3,128,512]{3,2,1,0:T(8,128)}, f32[128,512]{1,0:T(8,128)}) custom-call(bf16[3136,128]{1,0:T(8,128)(2,1)S(1)} %get-tuple-element.12.z, bf16[28,28,512]{2,1,0:T(8,128)(2,1)S(1)} %get-tuple-element.13.dx, f32[3,3,128,512]{3,2,1,0:T(8,128)S(1)} %get-tuple-element.14.dw, ...), custom_call_target="tpu_custom_call" | custom-call | tf_op jit(solution)/shard_map/pallas_call | solution.py:689

commit v4 on v3

--- a/solution.py
+++ b/solution.py
@@ -447,7 +447,7 @@
                     g_copy(o).start()
                 z_out[...] = zf[...].astype(BF)
 
-            inner_work = {1: lambda: far_grad(0), 3: lambda: far_grad(1), LATE: rest}
+            inner_work = {3: lambda: far_grad(0), 5: lambda: far_grad(1), LATE: rest}
             all_reduce(NEARS // 2, W3, p_wait, lambda k: None, {LATE: rest}, inner_work, ahead=2)
         with jax.named_scope("s1_out"):
             for idx, i in enumerate(NEAR):
@@ -556,25 +556,25 @@
         contract = (((1,), (1,)), ((), ()))
 
         def dx_tile(t, c):
-            h0 = t * HT
+            h0 = t * 2 * HT
             total = None
             for j in (1, 0, 2):
                 d = None
                 for i in range(3):
-                    lhs = gp[pl.ds(h0 + 2 - i, HT)].reshape(M, C)
+                    lhs = gp[pl.ds(h0 + 2 - i, 2 * HT)].reshape(2 * M, C)
                     p = lax.dot_general(lhs, w0[i, j].reshape(C, C), contract, preferred_element_type=F32)
                     d = p if d is None else d + p
                 if j == 1:
-                    d += lax.dot_general(gsp[pl.ds(h0, HT)].reshape(M, C), s0[...].reshape(C, C), contract, preferred_element_type=F32)
+                    d += lax.dot_general(gsp[pl.ds(h0, 2 * HT)].reshape(2 * M, C), s0[...].reshape(C, C), contract, preferred_element_type=F32)
                 else:
-                    d = pltpu.roll(d, M - 1 if j == 0 else 1, 0)
+                    d = pltpu.roll(d, 2 * M - 1 if j == 0 else 1, 0)
                 total = d if total is None else total + d
-            dx_out[pl.ds(h0, HT)] = total.astype(BF).reshape(HT, WP, C)[:, :HW, :]
+            dx_out[pl.ds(h0, 2 * HT)] = total.astype(BF).reshape(2 * HT, WP, C)[:, :HW, :]
             return c
 
         with jax.named_scope("s0_dx"):
             lax.fori_loop(0, HW, build, 0)
-            lax.fori_loop(0, NT, dx_tile, 0)
+            lax.fori_loop(0, NT // 2, dx_tile, 0)
 
         sent("a", xl.at[0])
         sent("x", xl.at[0, pl.ds(0, CROSS)])

time: 89.6 us -> 91.6 us (1.022)
  the two profiles are of different devices: /device:TPU:0 before, /device:TPU:17 now
where the time goes in v4:
time: 91.6 us; the launch traced here: 91.5 us
  Pallas kernels  90.7 us (99%)
    pallas_call x1, Pallas kernels, device_step(): call(act_in[0, 0], w_conv[0], w_short[0], gamma, beta, gamma_s, grads)  88.6 us
    pallas_call x1, Pallas kernels, device_step(): pl.pallas_call(place_kernel, out_shape=tuple((jax.ShapeDtypeStruct(a.shap...  2.1 us

profile of v4, /device:TPU:17, one launch (start us, length us, event | category | flops | bytes accessed | tf_op | source)
XLA Modules:
  0.0 91.5 jit_solution(18264022178783558884)
XLA Ops:
  0.6 88.6 %shard_map.102 = (bf16[3136,128]{1,0:T(8,128)(2,1)S(1)}, bf16[28,28,512]{2,1,0:T(8,128)(2,1)S(1)}, f32[3,3,128,512]{3,2,1,0:T(8,128)S(1)}, f32[128,512]{1,0:T(8,128)S(1)}) custom-call(bf16[28,28,512]{2,1,0:T(8,128)(2,1)} %bitcast.13, bf16[3,3,128,512]{3,2,1,0:T(8,128)(2,1)} %bitcast.12, bf16[128,512]{1,0:T(8,128)(2,1)} %bitcast.15, f32[1,128]{1,0:T(1,128)} %gam.1, ...), custom_call_target="tpu_custom_call" | custom-call | tf_op jit(solution)/shard_map/pallas_call | solution.py:688
  89.2 2.1 %shard_map.103 = (bf16[3136,128]{1,0:T(8,128)(2,1)}, bf16[28,28,512]{2,1,0:T(8,128)(2,1)}, f32[3,3,128,512]{3,2,1,0:T(8,128)}, f32[128,512]{1,0:T(8,128)}) custom-call(bf16[3136,128]{1,0:T(8,128)(2,1)S(1)} %get-tuple-element.12.z, bf16[28,28,512]{2,1,0:T(8,128)(2,1)S(1)} %get-tuple-element.13.dx, f32[3,3,128,512]{3,2,1,0:T(8,128)S(1)} %get-tuple-element.14.dw, ...), custom_call_target="tpu_custom_call" | custom-call | tf_op jit(solution)/shard_map/pallas_call | solution.py:689
